TPU v7x, 32 devices: a whole 2x2x4 slice. The times are simulated.
32 devices in a mesh: gx: 4 (over y, x), gy: 2 (over core), gz: 4 (over z).
Axes of the slice: x: 2, y: 2, z: 4, core: 2. Of those that a mesh axis runs over, the one named last changes fastest.
Arguments:
- start_block: float32 [64, 3, 8, 16, 512], P(None, None, 'gx', 'gy', 'gz'), may hold values from -6 to 6
- stiff_field: float32 [8, 16, 512], P('gx', 'gy', 'gz'), may hold values from 0.5 to 2
- shift_field: float32 [8, 16, 512], P('gx', 'gy', 'gz'), may hold values from 0.25 to 2
- mass_field: float32 [8, 16, 512], P('gx', 'gy', 'gz'), may hold values from 0.5 to 2
Outputs:
- modes: float32 [64, 3, 8, 16, 512], P(None, None, 'gx', 'gy', 'gz')
- ritz: float32 [64, 64], replicated
All inputs are finite; a program needn't handle non-finite values. Where the computation divides by a largest or mean magnitude, that divisor is 1e-20 or more.
Results may differ from a plain program's by a relative error of at most 0.0003.
Values sent between devices are 32-bit elements; how exact they have to be, the bound alone decides.
No kernel may reach another device: no remote copies, remote signals or barrier semaphores. Data moves between devices by JAX's collectives and lax.ppermute only.
A program may use at most 128 MiB of HBM per device.

v0:
```python
import jax
import jax.numpy as jnp
from jax import lax
from jax.sharding import PartitionSpec as P

ITERS = 2
FILTER = 4


def with_halo(x, sides, width):
    for axis, dim in sides:
        devices, length = (lax.axis_size(axis), x.shape[dim])
        up = [(i, (i + 1) % devices) for i in range(devices - 1)]
        down = [(j, i) for i, j in up]
        last = lax.slice_in_dim(x, length - width, length, axis=dim)
        initial = lax.slice_in_dim(x, 0, width, axis=dim)
        before = lax.ppermute(last, axis, up)
        after = lax.ppermute(initial, axis, down)
        x = jnp.concatenate([before, x, after], axis=dim)
    return x


def lower_solve(lower_mat, rhs):
    return lax.linalg.triangular_solve(lower_mat, rhs, left_side=True, lower=True)


def lower_trans_solve(lower_mat, rhs):
    return lax.linalg.triangular_solve(lower_mat, rhs, left_side=True, lower=True, transpose_a=True)


def hidot(left, right):
    return jnp.dot(left, right, precision=lax.Precision.HIGHEST, preferred_element_type=jnp.float32)


def gram_of(left, right):
    return hidot(left.reshape(left.shape[0], -1), right.reshape(right.shape[0], -1).T)


def combine(coeffs, vectors):
    flat = hidot(coeffs.T, vectors.reshape(vectors.shape[0], -1))
    return flat.reshape((coeffs.shape[1],) + vectors.shape[1:])


def crop_one(field):
    return field[..., 1:-1, 1:-1, 1:-1]


def offset_view(field, step_x, step_y, step_z):
    size_x, size_y, size_z = (field.shape[-3], field.shape[-2], field.shape[-1])
    return field[
        ...,
        1 + step_x : size_x - 1 + step_x,
        1 + step_y : size_y - 1 + step_y,
        1 + step_z : size_z - 1 + step_z,
    ]


def stiffness_local(padded_field, padded_stiff, center_stiff, center_shift):
    interior = crop_one(padded_field)
    offsets = ((1, 0, 0), (-1, 0, 0), (0, 1, 0), (0, -1, 0), (0, 0, 1), (0, 0, -1))
    beside_all = None
    for step_x, step_y, step_z in offsets:
        term = offset_view(padded_stiff, step_x, step_y, step_z) * offset_view(
            padded_field, step_x, step_y, step_z
        )
        beside_all = term if beside_all is None else beside_all + term
    laplace = 6.0 * (crop_one(padded_stiff) * interior) - beside_all
    summed = jnp.sum(interior, axis=1, keepdims=True)
    return center_stiff * laplace + center_shift * (interior + 0.5 * summed)


def ritz_filter(pencil_k, pencil_m, mode_count):
    factor = jnp.linalg.cholesky(pencil_m)
    partial_value = lower_solve(factor, pencil_k)
    reduced = lower_solve(factor, partial_value.T).T
    gershgorin = jnp.max(jnp.sum(jnp.abs(reduced), axis=1))
    search = factor.T[:, :mode_count]
    for sweep_index in range(FILTER):
        search = search - hidot(reduced, search) / gershgorin
    correlation = hidot(search.T, search)
    small_factor = jnp.linalg.cholesky(correlation)
    orthonormal = lower_solve(small_factor, search.T).T
    coeffs = lower_trans_solve(factor, orthonormal)
    ritz_matrix = hidot(orthonormal.T, hidot(reduced, orthonormal))
    return (coeffs, ritz_matrix)


def start_sums(start_block, mass_field, start_image, dof_count):
    mass_gram, stiff_gram = lax.psum(
        (gram_of(start_block, mass_field * start_block), gram_of(start_block, start_image)),
        ("gx", "gy", "gz"),
    )
    return (mass_gram / dof_count, stiff_gram / dof_count)


def normalize(factor, field):
    return lower_solve(factor, field.reshape(field.shape[0], -1)).reshape(field.shape)


def local(start_block, stiff_field, shift_field, mass_field):
    count = start_block.shape[0]
    dof_count = (
        3.0 * stiff_field.size * lax.axis_size("gx") * lax.axis_size("gy") * lax.axis_size("gz")
    )
    joined = jnp.stack([stiff_field, shift_field, mass_field])
    padded_coef = with_halo(joined, (("gx", 1), ("gy", 2), ("gz", 3)), 2)
    wide_coef = crop_one(padded_coef)
    diagonal = 6.0 * stiff_field * stiff_field + 1.5 * shift_field

    def apply_stiff(field):
        padded = with_halo(field, (("gx", 2), ("gy", 3), ("gz", 4)), 1)
        return stiffness_local(padded, wide_coef[0], stiff_field, shift_field)

    start_image = apply_stiff(start_block)
    mass_gram, stiff_gram = start_sums(start_block, mass_field, start_image, dof_count)
    factor = jnp.linalg.cholesky(mass_gram)
    current = normalize(factor, start_block)
    stiff_image = normalize(factor, start_image)
    ritz_matrix = lower_solve(factor, lower_solve(factor, stiff_gram).T).T
    residual = (stiff_image - mass_field * combine(ritz_matrix, current)) / diagonal
    stiff_resid = apply_stiff(residual)
    previous = None
    for iteration in range(ITERS):
        if iteration > 0:
            residual = (stiff_image - mass_field * combine(ritz_matrix, current)) / diagonal
            stiff_resid = apply_stiff(residual)
            search_set = jnp.concatenate([current, residual, previous[0]], axis=0)
            image_set = jnp.concatenate([stiff_image, stiff_resid, previous[1]], axis=0)
        else:
            search_set = jnp.concatenate([current, residual], axis=0)
            image_set = jnp.concatenate([stiff_image, stiff_resid], axis=0)
        pencil_k, pencil_m = lax.psum(
            (gram_of(search_set, image_set), gram_of(search_set, mass_field * search_set)),
            ("gx", "gy", "gz"),
        )
        coeffs, ritz_matrix = ritz_filter(pencil_k / dof_count, pencil_m / dof_count, count)
        current = combine(coeffs, search_set)
        stiff_image = combine(coeffs, image_set)
        previous = (
            combine(coeffs[count:], search_set[count:]),
            combine(coeffs[count:], image_set[count:]),
        )
    return (current, ritz_matrix)


def solution(mesh):
    in_specs = (
        P(None, None, "gx", "gy", "gz"),
        P("gx", "gy", "gz"),
        P("gx", "gy", "gz"),
        P("gx", "gy", "gz"),
    )
    out_specs = (P(None, None, "gx", "gy", "gz"), P())
    return jax.shard_map(local, mesh=mesh, in_specs=in_specs, out_specs=out_specs, check_vma=False)
```

profile of v0, /device:TPU:0, one launch (start us, length us, event | category | flops | bytes accessed | tf_op | source)
XLA Modules:
  0.0 744.3 jit_solution(5422652426399144735)
XLA Ops:
  7.9 4.9 collective-permute-start
  17.3 5.4 collective-permute-start.7
  33.1 5.3 collective-permute-done.7
  40.1 18.0 %collective-permute-done.6 = f32[64,3,1,8,128]{4,0,3,2,1:T(8,128)} collective-permute-done((f32[64,3,1,8,128]{4,0,3,2,1:T(8,128)}, f32[64,3,1,8,128]{4,0,3,2,1:T(8,128)}, u32[]{:S(2)}, u32[]{:S(2)}) %collective-permute-start.6) | collective-permute-done | bytes 786464 | tf_op jit(solution)/shard_map/ppermute | solution.py:18
  89.2 5.4 collective-permute-start.11
  103.1 5.7 fusion.61
  112.7 40.4 %all-reduce.5 = (f32[64,64]{0,1:T(8,128)S(1)}, f32[64,64]{0,1:T(8,128)S(1)}) all-reduce(f32[64,64]{0,1:T(8,128)S(1)} %copy-done.35, f32[64,64]{0,1:T(8,128)S(1)} %convolution_bitcast_fusion.3), channel_id=1, replica_groups=mesh['gx'=4,'gy'=2,'gz'=4] {'gx','gy','gz'}, use_global_device_ids=true, to_apply=%region_0.0 | all-reduce | flops 8192 | bytes 65536 | tf_op jit(solution)/shard_map/psum | solution.py:89
  153.2 5.8 cholesky.214
  160.4 4.9 custom-call.49
  178.8 4.8 collective-permute-start.13
  183.7 16.4 %collective-permute-done.12 = f32[64,3,1,8,128]{4,0,3,2,1:T(8,128)S(1)} collective-permute-done((f32[64,3,1,8,128]{4,0,3,2,1:T(8,128)S(1)}, f32[64,3,1,8,128]{4,0,3,2,1:T(8,128)S(1)}, u32[]{:S(2)}, u32[]{:S(2)}) %collective-permute-start.12) | collective-permute-done | bytes 786464 | tf_op jit(solution)/shard_map/ppermute | solution.py:18
  223.3 5.3 collective-permute-start.17
  259.6 128.5 %all-reduce.13.cloned.1.call-done = (f32[128,128]{0,1:T(8,128)}, f32[128,128]{0,1:T(8,128)}) async-done(((f32[128,128]{0,1:T(8,128)}, f32[128,128]{0,1:T(8,128)}), (f32[128,128]{0,1:T(8,128)}, f32[128,128]{0,1:T(8,128)})) %all-reduce.13.cloned.1.call-update) | async-done | bytes 131088 | tf_op jit(solution)/shard_map/psum | solution.py:132
  389.9 11.7 %cholesky.95 = f32[128,128]{1,0:T(8,128)S(1)} custom-call(f32[128,128]{1,0:T(8,128)S(1)} %fusion.124), custom_call_target="Cholesky" | custom-call | tf_op jit(solution)/shard_map/jit(cholesky)/cholesky | solution.py:73
  403.0 9.8 %custom-call.40 = f32[1,128,128]{1,2,0:T(8,128)S(1)} custom-call(f32[1,128,128]{2,1,0:T(8,128)S(1)} %get-tuple-element.101), custom_call_target="InvertDiagBlocksLowerTriangular" | custom-call | tf_op jit(solution)/shard_map/triangular_solve | solution.py:28
  418.5 5.8 cholesky.225
  425.7 4.9 custom-call.41
  436.8 5.9 fusion.177
  445.0 4.6 collective-permute-start.19
  459.9 6.2 collective-permute-done.18
  470.7 4.8 fusion.83
  489.0 5.2 collective-permute-start.23
  503.3 4.6 fusion.33
  507.9 4.6 fusion.80
  517.8 137.8 %all-reduce.11.cloned.1.call-done = (f32[192,192]{0,1:T(8,128)}, f32[192,192]{0,1:T(8,128)}) async-done(((f32[192,192]{0,1:T(8,128)}, f32[192,192]{0,1:T(8,128)}), (f32[192,192]{0,1:T(8,128)}, f32[192,192]{0,1:T(8,128)})) %all-reduce.11.cloned.1.call-update) | async-done | bytes 294928 | tf_op jit(solution)/shard_map/psum | solution.py:132
  657.7 11.7 %cholesky.155 = f32[128,128]{1,0:T(8,128)S(1)} custom-call(f32[128,128]{1,0:T(8,128)S(1)} %cholesky.245), custom_call_target="Cholesky" | custom-call | tf_op jit(solution)/shard_map/jit(cholesky)/cholesky | solution.py:73
  669.5 9.8 %custom-call.42 = f32[1,128,128]{1,2,0:T(8,128)S(1)} custom-call(f32[1,128,128]{2,1,0:T(8,128)S(1)} %get-tuple-element.99), custom_call_target="InvertDiagBlocksLowerTriangular" | custom-call | tf_op jit(solution)/shard_map/jit(cholesky)/cholesky | solution.py:73
  679.7 6.0 cholesky.169
  688.5 19.7 %custom-call.43 = f32[2,128,128]{1,2,0:T(8,128)S(1)} custom-call(f32[2,128,128]{2,1,0:T(8,128)S(1)} %pad_maximum_fusion.72), custom_call_target="InvertDiagBlocksLowerTriangular" | custom-call | tf_op jit(solution)/shard_map/triangular_solve | solution.py:28
  714.9 5.8 cholesky.236
  722.1 4.9 custom-call.44
  729.0 6.2 fusion.10
  (269 shorter events, 206.6 us)
Async XLA Ops:
  7.2 381.0 %all-reduce.13.cloned.1.call-start = ((), (), s32[]{:S(2)}) async-start(), calls=%async_computation.1 | async-start | bytes 262144 | tf_op jit(solution)/shard_map/psum | solution.py:132
  7.9 20.6 %collective-permute-start = (f32[3,2,8,128]{3,2,1,0:T(8,128)S(1)}, f32[3,2,8,128]{3,2,1,0:T(8,128)S(1)}, u32[]{:S(2)}, u32[]{:S(2)}) collective-permute-start(f32[3,2,8,128]{3,2,1,0:T(8,128)S(1)} %pad_maximum_fusion.78), channel_id=1, source_target_pairs={{0,8},{8,16},{16,24},{1,9},{9,17},{17,25},{2,10},{10,18},{18,26},{... | collective-permute-start | bytes 73736 | tf_op jit(solution)/shard_map/ppermute | solution.py:17
  12.8 15.8 %collective-permute-start.1 = (f32[3,2,8,128]{3,2,1,0:T(8,128)S(1)}, f32[3,2,8,128]{3,2,1,0:T(8,128)S(1)}, u32[]{:S(2)}, u32[]{:S(2)}) collective-permute-start(f32[3,2,8,128]{3,2,1,0:T(8,128)S(1)} %pad_maximum_fusion.78), channel_id=1, source_target_pairs={{8,0},{16,8},{24,16},{9,1},{17,9},{25,17},{10,2},{18,10},{26,18},{... | collective-permute-start | bytes 73736 | tf_op jit(solution)/shard_map/ppermute | solution.py:18
  17.3 21.1 %collective-permute-start.7 = (f32[64,3,1,8,128]{4,0,3,2,1:T(8,128)}, f32[64,3,1,8,128]{4,0,3,2,1:T(8,128)}, u32[]{:S(2)}, u32[]{:S(2)}) collective-permute-start(f32[64,3,1,8,128]{4,0,3,2,1:T(8,128)} %get-tuple-element.91), channel_id=1, source_target_pairs={{0,8},{8,16},{16,24},{1,9},{9,17},{17,25},{2,10},{10,18},{18,26},{... | collective-permute-start | bytes 2359304 | tf_op jit(solution)/shard_map/ppermute | solution.py:17
  22.7 35.4 %collective-permute-start.6 = (f32[64,3,1,8,128]{4,0,3,2,1:T(8,128)}, f32[64,3,1,8,128]{4,0,3,2,1:T(8,128)}, u32[]{:S(2)}, u32[]{:S(2)}) collective-permute-start(f32[64,3,1,8,128]{4,0,3,2,1:T(8,128)} %get-tuple-element.90), channel_id=1, source_target_pairs={{8,0},{16,8},{24,16},{9,1},{17,9},{25,17},{10,2},{18,10},{26,18},{... | collective-permute-start | bytes 2359304 | tf_op jit(solution)/shard_map/ppermute | solution.py:18
  28.6 3.2 collective-permute-start.2
  29.9 3.1 collective-permute-start.3
  59.3 16.0 %copy-start.5 = (f32[64,3,4,8,128]{4,0,3,2,1:T(8,128)}, f32[64,3,4,8,128]{4,0,3,2,1:T(8,128)S(1)}, u32[]{:S(2)}) copy-start(f32[64,3,4,8,128]{4,0,3,2,1:T(8,128)S(1)} %constant_dynamic-update-slice_fusion) | copy-start | bytes 9437188
  59.3 15.2 %copy-start.32 = (f32[3,2,8,128]{3,2,1,0:T(8,128)S(1)}, f32[3,2,8,128]{3,2,1,0:T(8,128)}, u32[]{:S(2)}) copy-start(f32[3,2,8,128]{3,2,1,0:T(8,128)} %copy-done.31) | copy-start | bytes 73732
  59.4 15.9 %collective-permute-start.8 = (f32[64,3,4,1,128]{4,0,3,2,1:T(8,128)S(1)}, f32[64,3,4,1,128]{4,0,3,2,1:T(8,128)S(1)}, u32[]{:S(2)}, u32[]{:S(2)}) collective-permute-start(f32[64,3,4,1,128]{4,0,3,2,1:T(8,128)S(1)} %get-tuple-element.82), channel_id=1, source_target_pairs={{4,0},{5,1},{6,2},{7,3},{12,8},{13,9},{14,10},{15,11},{20,16},{21,... | collective-permute-start | bytes 1179656 | tf_op jit(solution)/shard_map/ppermute | solution.py:18
  60.8 14.5 %collective-permute-start.9 = (f32[64,3,4,1,128]{4,0,3,2,1:T(8,128)S(1)}, f32[64,3,4,1,128]{4,0,3,2,1:T(8,128)S(1)}, u32[]{:S(2)}, u32[]{:S(2)}) collective-permute-start(f32[64,3,4,1,128]{4,0,3,2,1:T(8,128)S(1)} %get-tuple-element.81), channel_id=1, source_target_pairs={{0,4},{1,5},{2,6},{3,7},{8,12},{9,13},{10,14},{11,15},{16,20},{17,... | collective-permute-start | bytes 1179656 | tf_op jit(solution)/shard_map/ppermute | solution.py:17
  64.0 6.1 collective-permute-start.4
  67.5 7.0 collective-permute-start.5
  84.5 11.9 %collective-permute-start.10 = (f32[64,3,4,10,1]{0,2,4,3,1:T(4,128)}, f32[64,3,4,10,1]{0,2,4,3,1:T(4,128)}, u32[]{:S(2)}, u32[]{:S(2)}) collective-permute-start(f32[64,3,4,10,1]{0,2,4,3,1:T(4,128)} %copy.129), channel_id=1, source_target_pairs={{1,0},{2,1},{3,2},{5,4},{6,5},{7,6},{9,8},{10,9},{11,10},{13,12},{... | collective-permute-start | bytes 92168 | tf_op jit(solution)/shard_map/ppermute | solution.py:18
  89.2 10.5 %collective-permute-start.11 = (f32[64,3,4,10,1]{0,2,4,3,1:T(4,128)}, f32[64,3,4,10,1]{0,2,4,3,1:T(4,128)}, u32[]{:S(2)}, u32[]{:S(2)}) collective-permute-start(f32[64,3,4,10,1]{0,2,4,3,1:T(4,128)} %copy.131), channel_id=1, source_target_pairs={{0,1},{1,2},{2,3},{4,5},{5,6},{6,7},{8,9},{9,10},{10,11},{12,13},{... | collective-permute-start | bytes 92168 | tf_op jit(solution)/shard_map/ppermute | solution.py:17
  177.5 22.6 %collective-permute-start.12 = (f32[64,3,1,8,128]{4,0,3,2,1:T(8,128)S(1)}, f32[64,3,1,8,128]{4,0,3,2,1:T(8,128)S(1)}, u32[]{:S(2)}, u32[]{:S(2)}) collective-permute-start(f32[64,3,1,8,128]{4,0,3,2,1:T(8,128)S(1)} %get-tuple-element.89), channel_id=1, source_target_pairs={{8,0},{16,8},{24,16},{9,1},{17,9},{25,17},{10,2},{18,10},{26,18},{... | collective-permute-start | bytes 2359304 | tf_op jit(solution)/shard_map/ppermute | solution.py:18
  178.8 21.3 %collective-permute-start.13 = (f32[64,3,1,8,128]{4,0,3,2,1:T(8,128)S(1)}, f32[64,3,1,8,128]{4,0,3,2,1:T(8,128)S(1)}, u32[]{:S(2)}, u32[]{:S(2)}) collective-permute-start(f32[64,3,1,8,128]{4,0,3,2,1:T(8,128)S(1)} %get-tuple-element.88), channel_id=1, source_target_pairs={{0,8},{8,16},{16,24},{1,9},{9,17},{17,25},{2,10},{10,18},{18,26},{... | collective-permute-start | bytes 2359304 | tf_op jit(solution)/shard_map/ppermute | solution.py:17
  200.2 9.4 %collective-permute-start.14 = (f32[64,3,4,1,128]{4,0,3,2,1:T(8,128)S(1)}, f32[64,3,4,1,128]{4,0,3,2,1:T(8,128)S(1)}, u32[]{:S(2)}, u32[]{:S(2)}) collective-permute-start(f32[64,3,4,1,128]{4,0,3,2,1:T(8,128)S(1)} %get-tuple-element.80), channel_id=1, source_target_pairs={{4,0},{5,1},{6,2},{7,3},{12,8},{13,9},{14,10},{15,11},{20,16},{21,... | collective-permute-start | bytes 1179656 | tf_op jit(solution)/shard_map/ppermute | solution.py:18
  201.5 8.1 %collective-permute-start.15 = (f32[64,3,4,1,128]{4,0,3,2,1:T(8,128)S(1)}, f32[64,3,4,1,128]{4,0,3,2,1:T(8,128)S(1)}, u32[]{:S(2)}, u32[]{:S(2)}) collective-permute-start(f32[64,3,4,1,128]{4,0,3,2,1:T(8,128)S(1)} %get-tuple-element.79), channel_id=1, source_target_pairs={{0,4},{1,5},{2,6},{3,7},{8,12},{9,13},{10,14},{11,15},{16,20},{17,... | collective-permute-start | bytes 1179656 | tf_op jit(solution)/shard_map/ppermute | solution.py:17
  218.6 13.8 %collective-permute-start.16 = (f32[64,3,4,10,1]{0,2,4,3,1:T(4,128)}, f32[64,3,4,10,1]{0,2,4,3,1:T(4,128)}, u32[]{:S(2)}, u32[]{:S(2)}) collective-permute-start(f32[64,3,4,10,1]{0,2,4,3,1:T(4,128)} %copy.142), channel_id=1, source_target_pairs={{1,0},{2,1},{3,2},{5,4},{6,5},{7,6},{9,8},{10,9},{11,10},{13,12},{... | collective-permute-start | bytes 92168 | tf_op jit(solution)/shard_map/ppermute | solution.py:18
  223.3 12.5 %collective-permute-start.17 = (f32[64,3,4,10,1]{0,2,4,3,1:T(4,128)}, f32[64,3,4,10,1]{0,2,4,3,1:T(4,128)}, u32[]{:S(2)}, u32[]{:S(2)}) collective-permute-start(f32[64,3,4,10,1]{0,2,4,3,1:T(4,128)} %copy.144), channel_id=1, source_target_pairs={{0,1},{1,2},{2,3},{4,5},{5,6},{6,7},{8,9},{9,10},{10,11},{12,13},{... | collective-permute-start | bytes 92168 | tf_op jit(solution)/shard_map/ppermute | solution.py:17
  250.2 405.3 %all-reduce.11.cloned.1.call-start = ((), (), s32[]{:S(2)}) async-start(), calls=%async_computation | async-start | bytes 786432 | tf_op jit(solution)/shard_map/psum | solution.py:132
  259.6 171.6 %copy-start.8 = (f32[64,6144]{1,0:T(8,128)S(1)}, f32[64,6144]{1,0:T(8,128)}, u32[]{:S(2)}) copy-start(f32[64,6144]{1,0:T(8,128)} %get-tuple-element.111) | copy-start | bytes 4718596
  433.1 22.1 %copy-start.1 = (f32[64,6144]{1,0:T(8,128)}, f32[64,6144]{1,0:T(8,128)S(1)}, u32[]{:S(2)}) copy-start(f32[64,6144]{1,0:T(8,128)S(1)} %fusion.16) | copy-start | bytes 4718596
  443.7 22.3 %collective-permute-start.18 = (f32[64,3,1,8,128]{4,0,3,2,1:T(8,128)S(1)}, f32[64,3,1,8,128]{4,0,3,2,1:T(8,128)S(1)}, u32[]{:S(2)}, u32[]{:S(2)}) collective-permute-start(f32[64,3,1,8,128]{4,0,3,2,1:T(8,128)S(1)} %get-tuple-element.84), channel_id=1, source_target_pairs={{8,0},{16,8},{24,16},{9,1},{17,9},{25,17},{10,2},{18,10},{26,18},{... | collective-permute-start | bytes 2359304 | tf_op jit(solution)/shard_map/ppermute | solution.py:18
  445.0 21.0 %collective-permute-start.19 = (f32[64,3,1,8,128]{4,0,3,2,1:T(8,128)S(1)}, f32[64,3,1,8,128]{4,0,3,2,1:T(8,128)S(1)}, u32[]{:S(2)}, u32[]{:S(2)}) collective-permute-start(f32[64,3,1,8,128]{4,0,3,2,1:T(8,128)S(1)} %get-tuple-element.83), channel_id=1, source_target_pairs={{0,8},{8,16},{16,24},{1,9},{9,17},{17,25},{2,10},{10,18},{18,26},{... | collective-permute-start | bytes 2359304 | tf_op jit(solution)/shard_map/ppermute | solution.py:17
  451.5 19.2 %copy-start.15 = (f32[64,3,2,8,128]{4,0,3,2,1:T(8,128)}, f32[64,3,2,8,128]{4,0,3,2,1:T(8,128)S(1)}, u32[]{:S(2)}) copy-start(f32[64,3,2,8,128]{4,0,3,2,1:T(8,128)S(1)} %fusion.73) | copy-start | bytes 4718596
  466.1 9.4 %collective-permute-start.20 = (f32[64,3,4,1,128]{4,0,3,2,1:T(8,128)S(1)}, f32[64,3,4,1,128]{4,0,3,2,1:T(8,128)S(1)}, u32[]{:S(2)}, u32[]{:S(2)}) collective-permute-start(f32[64,3,4,1,128]{4,0,3,2,1:T(8,128)S(1)} %get-tuple-element.78), channel_id=1, source_target_pairs={{4,0},{5,1},{6,2},{7,3},{12,8},{13,9},{14,10},{15,11},{20,16},{21,... | collective-permute-start | bytes 1179656 | tf_op jit(solution)/shard_map/ppermute | solution.py:18
  467.4 8.1 %collective-permute-start.21 = (f32[64,3,4,1,128]{4,0,3,2,1:T(8,128)S(1)}, f32[64,3,4,1,128]{4,0,3,2,1:T(8,128)S(1)}, u32[]{:S(2)}, u32[]{:S(2)}) collective-permute-start(f32[64,3,4,1,128]{4,0,3,2,1:T(8,128)S(1)} %get-tuple-element.77), channel_id=1, source_target_pairs={{0,4},{1,5},{2,6},{3,7},{8,12},{9,13},{10,14},{11,15},{16,20},{17,... | collective-permute-start | bytes 1179656 | tf_op jit(solution)/shard_map/ppermute | solution.py:17
  484.2 12.2 %collective-permute-start.22 = (f32[64,3,4,10,1]{0,2,4,3,1:T(4,128)}, f32[64,3,4,10,1]{0,2,4,3,1:T(4,128)}, u32[]{:S(2)}, u32[]{:S(2)}) collective-permute-start(f32[64,3,4,10,1]{0,2,4,3,1:T(4,128)} %copy.158), channel_id=1, source_target_pairs={{1,0},{2,1},{3,2},{5,4},{6,5},{7,6},{9,8},{10,9},{11,10},{13,12},{... | collective-permute-start | bytes 92168 | tf_op jit(solution)/shard_map/ppermute | solution.py:18
  489.0 10.9 %collective-permute-start.23 = (f32[64,3,4,10,1]{0,2,4,3,1:T(4,128)}, f32[64,3,4,10,1]{0,2,4,3,1:T(4,128)}, u32[]{:S(2)}, u32[]{:S(2)}) collective-permute-start(f32[64,3,4,10,1]{0,2,4,3,1:T(4,128)} %copy.160), channel_id=1, source_target_pairs={{0,1},{1,2},{2,3},{4,5},{5,6},{6,7},{8,9},{9,10},{10,11},{12,13},{... | collective-permute-start | bytes 92168 | tf_op jit(solution)/shard_map/ppermute | solution.py:17
  655.5 32.8 %copy-start.30 = (f32[128,64]{1,0:T(8,128)S(1)}, f32[128,64]{1,0:T(8,128)}, u32[]{:S(2)}) copy-start(f32[128,64]{1,0:T(8,128)} %pad_convert_fusion) | copy-start | bytes 98308
  (32 other events, 154.9 us)
Sparse Core Ops, SparseCore 0:
  250.4 137.7 all-reduce.12
  512.7 142.8 all-reduce.10
where the time goes:
time: 752 us; the launch traced here: 744 us
  waiting for transfers between devices  318 us (42%)
  other arithmetic  146 us (19%)
  local copies, waits for them, and re-layouts  95.4 us (13%)
  starting transfers between devices  65.8 us (9%)
  matrix products  61.6 us (8%)
  blocking collectives  40.4 us (5%)
  between operations  16.8 us (2%)
    psum x2, waiting for transfers between devices, local(): lax.psum((gram_of(search_set, image_set), gram_of(search_set, mass_field...  266 us
    dot_general x27, matrix products, hidot(): jnp.dot(left, right, precision=lax.Precision.HIGHEST, preferred_element_t...  51.1 us
    ppermute x12, starting transfers between devices, with_halo(): before = lax.ppermute(last, axis, up)  50 us
    ppermute x12, waiting for transfers between devices, with_halo(): after = lax.ppermute(initial, axis, down)  46.2 us
    another operation x10, other arithmetic, ritz_filter(): factor = jnp.linalg.cholesky(pencil_m)  41.2 us
    psum x1, blocking collectives, start_sums(): lax.psum((gram_of(start_block, mass_field * start_block), gram_of(start_b...  40.4 us
    another operation x7, other arithmetic, lower_trans_solve(): lax.linalg.triangular_solve(lower_mat, rhs, left_side=True, lower=True, t...  30.2 us
    slice x7, local copies, waits for them, and re-layouts, with_halo(): initial = lax.slice_in_dim(x, 0, width, axis=dim)  24.8 us
  transfers between devices with their start and end apart: 26, of which 9 were waited for; matrix products, arithmetic and copies ran while one was open for 10% of the time, Pallas kernels for 0%

commit v1 on v0

v1 whole, which is shorter than its diff:
```python
import functools

import jax
import jax.numpy as jnp
from jax import lax
from jax.experimental import pallas as pl
from jax.experimental.pallas import tpu as pltpu
from jax.sharding import PartitionSpec as P

FILTER = 4
AXES = ("gx", "gy", "gz")
F32 = jnp.float32
BF16 = jnp.bfloat16
G_ROW, E_ROW, RHO_ROW, W_ROW, ID_ROW, GD_ROW = range(6)


def dg(a, b, ca, cb):
    return lax.dot_general(a, b, (((ca,), (cb,)), ((), ())),
                           precision=lax.Precision.HIGHEST, preferred_element_type=F32)


def nn(a, b):
    return dg(a, b, 1, 0)


def nt(a, b):
    return dg(a, b, 1, 1)


def lane_eye(rows, lanes, shift):
    return (lax.broadcasted_iota(jnp.int32, (rows, lanes), 1)
            == lax.broadcasted_iota(jnp.int32, (rows, lanes), 0) + shift).astype(F32)


def chol_inverse(mat):
    n = mat.shape[0]
    panels = n // 8
    width = 2 * n
    rows = [jnp.concatenate([mat[8 * p:8 * p + 8, :], lane_eye(8, n, 8 * p)], axis=1) for p in range(panels)]
    sub = lax.broadcasted_iota(jnp.int32, (8, width), 0)
    out = []
    for p in range(panels):
        w = rows[p]
        spread = lambda v, k: jnp.broadcast_to(v[:, 8 * p + k:8 * p + k + 1], (8, width))
        d = [spread(w, k) for k in range(8)]
        rest = {q: [spread(rows[q], k) for k in range(8)] for q in range(p + 1, panels)}
        done = jnp.zeros((8, width), F32)
        for k in range(8):
            row_of = lambda v: jnp.broadcast_to(v[k:k + 1, :], (8, width))
            pivot = row_of(d[k])
            inv = 1.0 / pivot
            at_k = sub == k
            w_row = row_of(w)
            done = jnp.where(at_k, w_row * lax.rsqrt(pivot), done)
            scaled = w_row * inv
            factor = d[k]
            w = jnp.where(at_k, scaled, w - factor * scaled)
            for j in range(k + 1, 8):
                d_row = row_of(d[j]) * inv
                d[j] = jnp.where(at_k, d_row, d[j] - factor * d_row)
        out.append(done)
        for q in range(p + 1, panels):
            for k in range(8):
                rows[q] = rows[q] - rest[q][k] * jnp.broadcast_to(w[k:k + 1, :], (8, width))
    return jnp.concatenate(out, axis=0)[:, n:]


def filtered(theta, h21, h22):
    n, m = theta.shape[0], h22.shape[0]
    h12 = h21.T
    whole = jnp.concatenate([jnp.concatenate([h22, h21], axis=1), jnp.concatenate([h12, theta], axis=1)], axis=0)
    inv = 1.0 / jnp.max(jnp.sum(jnp.abs(whole), axis=1, keepdims=True))
    search = lane_eye(n, m + n, m) - whole[m:, :] * inv
    for _ in range(FILTER - 1):
        search = search - nn(search, whole) * inv
    q = nn(chol_inverse(nt(search, search)), search)
    return q[:, m:], q[:, :m], nt(nn(q, whole), q)


def dense0_kernel(scale, gram_ref, coef_ref, theta_ref):
    v = gram_ref.shape[0]
    sbs = gram_ref[:, :v] * scale
    sks = gram_ref[:, v:] * scale
    li = chol_inverse(sbs)
    theta = nt(nn(li, sks), li)
    coef_ref[:, :v] = li
    coef_ref[:, v:] = -nn(theta, li)
    theta_ref[...] = theta


def dense1_kernel(scale, gram_ref, coef_ref, theta_ref, coef1_ref, theta1_ref):
    v = gram_ref.shape[0]
    li = coef_ref[:, :v]
    theta = theta_ref[...]
    rbs, rks, rbr, rkr = [gram_ref[:, i * v:(i + 1) * v] * scale for i in (0, 2, 1, 3)]
    lrx = nt(rbs, li)
    arx = nt(rks, li)
    jr = chol_inverse(rbr - nt(lrx, lrx))
    t = arx - nn(lrx, theta)
    f = rkr - nt(lrx, arx) - nt(t, lrx)
    h21 = nn(jr, t)
    h22 = nt(nn(jr, f), jr)
    qz, qy, ritz = filtered(theta, h21, h22)
    b = nn(qy, jr)
    a = nn(qz - nn(b, lrx), li)
    coef1_ref[:, :v] = a
    coef1_ref[:, v:2 * v] = b
    coef1_ref[:, 2 * v:3 * v] = -nn(ritz, a)
    coef1_ref[:, 3 * v:] = -nn(ritz, b)
    theta1_ref[...] = ritz


def previous_kernel(scale, gram_ref, coef1_ref, out_ref):
    v = gram_ref.shape[0]
    ab = coef1_ref[:, :2 * v]
    b = coef1_ref[:, v:2 * v]
    for i in range(2):
        part = nn(b, gram_ref[:, 2 * i * v:2 * (i + 1) * v] * scale)
        out_ref[:, 2 * i * v:(2 * i + 1) * v] = nt(part, ab)
        out_ref[:, (2 * i + 1) * v:2 * (i + 1) * v] = nt(part[:, v:], b)


def dense2_kernel(scale, gram_ref, prev_ref, coef1_ref, theta1_ref, coef2_ref, theta2_ref):
    v = gram_ref.shape[0]
    both = coef1_ref[:, :2 * v]
    a = coef1_ref[:, :v]
    b = coef1_ref[:, v:2 * v]
    theta = theta1_ref[...]
    lpx, mpp, apx, app = [prev_ref[:, i * v:(i + 1) * v] for i in range(4)]
    lrx = nt(gram_ref[:, :2 * v] * scale, both)
    arx = nt(gram_ref[:, 2 * v:4 * v] * scale, both)
    mrp = nt(gram_ref[:, v:2 * v] * scale, b)
    arp = nt(gram_ref[:, 3 * v:4 * v] * scale, b)
    rbr = gram_ref[:, 4 * v:5 * v] * scale
    rkr = gram_ref[:, 5 * v:] * scale
    jr = chol_inverse(rbr - nt(lrx, lrx))
    low = nt(mrp.T - nt(lpx, lrx), jr)
    jp = chol_inverse(mpp - nt(lpx, lpx) - nt(low, low))
    jpr = -nn(jp, nn(low, jr))
    jb = jnp.concatenate([jnp.concatenate([jr, jnp.zeros((v, v), F32)], axis=1),
                          jnp.concatenate([jpr, jp], axis=1)], axis=0)
    lx = jnp.concatenate([lrx, lpx], axis=0)
    ax = jnp.concatenate([arx, apx], axis=0)
    ab = jnp.concatenate([jnp.concatenate([rkr, arp], axis=1),
                          jnp.concatenate([arp.T, app], axis=1)], axis=0)
    t = ax - nn(lx, theta)
    f = ab - nt(lx, ax) - nt(t, lx)
    h21 = nn(jb, t)
    h22 = nt(nn(jb, f), jb)
    qz, qy, ritz = filtered(theta, h21, h22)
    cb = nn(qy, jb)
    cx = qz - nn(cb, lx)
    coef2_ref[:, :v] = nn(cx, a)
    coef2_ref[:, v:2 * v] = nn(cx + cb[:, v:], b)
    coef2_ref[:, 2 * v:3 * v] = cb[:, :v]
    coef2_ref[:, 3 * v:] = jnp.zeros((v, v), F32)
    theta2_ref[...] = ritz


def split(value):
    high = value.astype(BF16)
    return high, (value - high.astype(F32)).astype(BF16)


def bdot(a, b, cb):
    return lax.dot_general(a, b, (((1,), (cb,)), ((), ())), preferred_element_type=F32)


def mix(coef_high, coef_both, blocks):
    v = coef_high.shape[0]
    pairs = [split(block) for block in blocks]
    high = jnp.concatenate([p[0] for p in pairs], axis=0)
    low = jnp.concatenate([p[1] for p in pairs], axis=0)
    main = bdot(coef_both, high, 0)
    return main[:v] + main[v:] + bdot(coef_high, low, 0)


class Grid:
    def __init__(self, shape):
        self.v, self.c, self.nx, self.ny, self.nz = shape
        self.blocks = self.c * self.nx * self.ny
        self.lanes = self.blocks * self.nz
        self.xface = self.c * self.ny * self.nz
        self.yface = self.c * self.nx * self.nz
        assert self.blocks < self.nz and self.nz % 128 == 0 and self.ny % 2 == 0
        assert self.nx * self.nz >= 1 and self.v % 16 == 0 and max(self.ny, self.nx) <= self.v

    def block(self, c, x, y):
        return (c * self.nx + x) * self.ny + y

    def at(self, j):
        return slice(j * self.nz, (j + 1) * self.nz)


def put_faces(gd, value, c, x, y, refs, edge):
    xlo, xhi, ylo, yhi = refs
    if x == 0:
        xlo[:gd.v, gd.at(c * gd.ny + y)] = value
    if x == gd.nx - 1:
        xhi[:gd.v, gd.at(c * gd.ny + y)] = value
    if y == 0:
        ylo[:gd.v, gd.at(c * gd.nx + x)] = value
    if y == gd.ny - 1:
        yhi[:gd.v, gd.at(c * gd.nx + x)] = value
    j = gd.block(c, x, y)
    lane = lax.broadcasted_iota(jnp.int32, value.shape, 1)
    low, high = edge
    rolled_low = value if j == 0 else pltpu.roll(value, j, 1)
    rolled_high = pltpu.roll(value, (j + 1) % gd.nz, 1)
    return (jnp.where(lane == j, rolled_low, low), jnp.where(lane == j, rolled_high, high))


def stencil(gd, get, halo, coef_ref, x, y):
    xb, xa, yb, ya, zb, za = halo
    row = lambda r, xx, yy: coef_ref[r:r + 1, gd.at(xx * gd.ny + yy)]
    scaled = lambda c, xx, yy: get(c, xx, yy) * row(G_ROW, xx, yy)
    g, e = row(G_ROW, x, y), row(E_ROW, x, y)
    values = [get(c, x, y) for c in range(gd.c)]
    half = 0.5 * functools.reduce(jnp.add, values)
    lane = lax.broadcasted_iota(jnp.int32, (gd.v, gd.nz), 1)
    out = []
    for c in range(gd.c):
        j = gd.block(c, x, y)
        h = values[c] * g
        face_x, face_y = gd.at(c * gd.ny + y), gd.at(c * gd.nx + x)
        near = scaled(c, x - 1, y) if x > 0 else xb[:gd.v, face_x]
        near = near + (scaled(c, x + 1, y) if x < gd.nx - 1 else xa[:gd.v, face_x])
        near = near + (scaled(c, x, y - 1) if y > 0 else yb[:gd.v, face_y])
        near = near + (scaled(c, x, y + 1) if y < gd.ny - 1 else ya[:gd.v, face_y])
        below = jnp.broadcast_to(zb[:gd.v, j:j + 1], h.shape)
        above = jnp.broadcast_to(za[:gd.v, j:j + 1], h.shape)
        near = near + jnp.where(lane == 0, below, pltpu.roll(h, 1, 1))
        near = near + jnp.where(lane == gd.nz - 1, above, pltpu.roll(h, gd.nz - 1, 1))
        out.append(g * (6.0 * h - near) + e * (values[c] + half))
    return out


def gram_of(left_both, right_high, right_low):
    v = left_both.shape[0] // 2
    main = bdot(left_both[...], right_high[...], 1)
    return main[:v] + main[v:] + bdot(left_both[:v, :], right_low[...], 1)


def pack_kernel(gd, s_ref, g_ref, e_ref, rho_ref, sm_ref, coef_ref, xlo, xhi, ylo, yhi, zlo, zhi):
    v, nz = gd.v, gd.nz
    coef_ref[...] = jnp.zeros(coef_ref.shape, F32)
    for ref, used in ((xlo, gd.xface), (xhi, gd.xface), (ylo, gd.yface), (yhi, gd.yface)):
        ref[:, used:] = jnp.zeros((v, nz), F32)
    w_lane = lax.broadcasted_iota(jnp.int32, (8, nz), 1)
    w_low = jnp.zeros((8, nz), F32)
    w_high = jnp.zeros((8, nz), F32)
    for x in range(gd.nx):
        for y in range(gd.ny):
            r = x * gd.ny + y
            g, e, rho = (ref[r:r + 1, :] for ref in (g_ref, e_ref, rho_ref))
            inverse = 1.0 / (6.0 * g * g + 1.5 * e)
            w = rho * inverse
            for i, value in enumerate((g, e, rho, w, inverse, g * inverse)):
                coef_ref[i:i + 1, gd.at(r)] = value
            if x == 0:
                xlo[y:y + 1, gd.xface:] = w
            if x == gd.nx - 1:
                xhi[y:y + 1, gd.xface:] = w
            if y == 0:
                ylo[x:x + 1, gd.yface:] = w
            if y == gd.ny - 1:
                yhi[x:x + 1, gd.yface:] = w
            wide = jnp.broadcast_to(w, (8, nz))
            for c in range(gd.c):
                j = gd.block(c, x, y)
                w_low = jnp.where(w_lane == j, pltpu.roll(wide, j, 1) if j else wide, w_low)
                w_high = jnp.where(w_lane == j, pltpu.roll(wide, (j + 1) % nz, 1), w_high)
    edge = (jnp.zeros((v, nz), F32), jnp.zeros((v, nz), F32))
    for c in range(gd.c):
        for x in range(gd.nx):
            for y in range(gd.ny):
                j = gd.block(c, x, y)
                value = s_ref[pl.ds(j, v, stride=gd.blocks), :]
                sm_ref[:, gd.at(j)] = value
                edge = put_faces(gd, value * coef_ref[G_ROW:G_ROW + 1, gd.at(x * gd.ny + y)], c, x, y,
                                 (xlo, xhi, ylo, yhi), edge)
    zlo[:v, :], zhi[:v, :] = edge
    zlo[v:, :] = w_low
    zhi[v:, :] = w_high


def image_kernel(gd, sm_ref, coef_ref, xb, xa, yb, ya, zb, za,
                 ks_ref, gram_ref, xlo, xhi, ylo, yhi, zlo, zhi, left, right_high, right_low):
    v = gd.v
    get = lambda c, x, y: sm_ref[:, gd.at(gd.block(c, x, y))]
    edge = (jnp.zeros((v, gd.nz), F32), jnp.zeros((v, gd.nz), F32))
    for x in range(gd.nx):
        for y in range(gd.ny):
            r = gd.at(x * gd.ny + y)
            images = stencil(gd, get, (xb, xa, yb, ya, zb, za), coef_ref, x, y)
            for c in range(gd.c):
                at = gd.at(gd.block(c, x, y))
                value = get(c, x, y)
                ks_ref[:, at] = images[c]
                edge = put_faces(gd, images[c] * coef_ref[GD_ROW:GD_ROW + 1, r], c, x, y, (xlo, xhi, ylo, yhi), edge)
                left[:v, at], left[v:, at] = split(value)
                for i, part in enumerate((value * coef_ref[RHO_ROW:RHO_ROW + 1, r], images[c])):
                    right_high[i * v:(i + 1) * v, at], right_low[i * v:(i + 1) * v, at] = split(part)
    zlo[...], zhi[...] = edge
    gram_ref[...] = gram_of(left, right_high, right_low)


def coefficients(coef_ref, both_ref):
    v = coef_ref.shape[0]
    both_ref[:v, :], both_ref[v:, :] = split(coef_ref[...])


def residual_kernel(gd, last, depth, *refs):
    v, nz = gd.v, gd.nz
    refs = list(refs)
    take = lambda n: [refs.pop(0) for _ in range(n)]
    (mix_ref, coef_ref) = take(2)
    images, vectors = take(depth), take(depth)
    image_halo = [take(6) for _ in range(depth)]
    vector_halo = [take(6) for _ in range(depth)]
    if last:
        r_ref, gram_ref = take(2)
        halo = take(6)
    else:
        r_ref, kr_ref, gram_ref = take(3)
        halo = take(6)
        faces = take(6)
    both, left, right_high, right_low = take(4)
    both[:v, :], both[v:, :] = split(mix_ref[...])
    mixed = lambda a, b: mix(both[:v, :], both[...], a + b)
    first = vector_halo[0]

    def interior(c, _):
        for i in range(gd.nx * gd.ny // 2):
            at = pl.ds(pl.multiple_of(c * gd.nx * gd.ny * nz + 2 * i * nz, 2 * nz), 2 * nz)
            row = slice(2 * i * nz, 2 * (i + 1) * nz)
            inverse, w = coef_ref[ID_ROW:ID_ROW + 1, row], coef_ref[W_ROW:W_ROW + 1, row]
            r_ref[:, at] = mixed([ref[:, at] * inverse for ref in images], [ref[:, at] * w for ref in vectors])
        return 0

    def xfaces(c, _):
        for side in range(2):
            for i in range(gd.ny // 2):
                at = pl.ds(pl.multiple_of(c * gd.ny * nz + 2 * i * nz, 2 * nz), 2 * nz)
                w = jnp.concatenate([first[side][k:k + 1, gd.xface:] for k in (2 * i, 2 * i + 1)], axis=1)
                halo[side][:, at] = mixed([h[side][:v, at] for h in image_halo],
                                          [h[side][:v, at] * w for h in vector_halo])
        return 0

    lax.fori_loop(0, gd.c, xfaces, 0)
    for side in (2, 3):
        for j in range(gd.c * gd.nx):
            at = gd.at(j)
            w = first[side][j % gd.nx:j % gd.nx + 1, gd.yface:]
            halo[side][:, at] = mixed([h[side][:v, at] for h in image_halo], [h[side][:v, at] * w for h in vector_halo])
    for side in (4, 5):
        w = first[side][v:v + 1, :]
        halo[side][...] = mixed([h[side][:v, :] for h in image_halo], [h[side][:v, :] * w for h in vector_halo])
    lax.fori_loop(0, gd.c, interior, 0)

    get = lambda c, x, y: r_ref[:, gd.at(gd.block(c, x, y))]
    edge = (jnp.zeros((v, nz), F32), jnp.zeros((v, nz), F32))
    for x in range(gd.nx):
        for y in range(gd.ny):
            r = gd.at(x * gd.ny + y)
            rho = coef_ref[RHO_ROW:RHO_ROW + 1, r]
            stiff = stencil(gd, get, halo, coef_ref, x, y)
            for c in range(gd.c):
                at = gd.at(gd.block(c, x, y))
                value = get(c, x, y)
                if not last:
                    kr_ref[:, at] = stiff[c]
                    edge = put_faces(gd, stiff[c] * coef_ref[GD_ROW:GD_ROW + 1, r], c, x, y, faces[:4], edge)
                left[:v, at], left[v:, at] = split(value)
                parts = [ref[:, at] * rho for ref in vectors] + [ref[:, at] for ref in images]
                place = depth if not last else 2 * depth
                parts.insert(place, value * rho)
                parts.append(stiff[c])
                for i, part in enumerate(parts):
                    right_high[i * v:(i + 1) * v, at], right_low[i * v:(i + 1) * v, at] = split(part)
    if not last:
        faces[4][...], faces[5][...] = edge
    gram_ref[...] = gram_of(left, right_high, right_low)


def final_kernel(gd, mix_ref, s_ref, r0_ref, r1_ref, out_ref, both):
    v, nz = gd.v, gd.nz
    k = 3 * v
    both[:v, :], both[v:, :] = split(mix_ref[...])
    high, pair = both[:v, :k], both[:, :k]
    for j in range(0, gd.blocks, 2):
        at = slice(j * nz, (j + 2) * nz)
        value = mix(high, pair, [s_ref[:, at], r0_ref[:, at], r1_ref[:, at]])
        out_ref[pl.ds(j, v, stride=gd.blocks), :] = value[:, :nz]
        out_ref[pl.ds(j + 1, v, stride=gd.blocks), :] = value[:, nz:]


def call(kernel, outs, args, scratch=(), flops=1 << 20, vmem=40 << 20):
    spec = pl.BlockSpec(memory_space=pltpu.VMEM)
    results = pl.pallas_call(
        kernel,
        out_shape=[jax.ShapeDtypeStruct(s, F32) for s in outs],
        in_specs=[spec] * len(args),
        out_specs=[spec] * len(outs),
        scratch_shapes=[pltpu.VMEM(s, d) for s, d in scratch],
        compiler_params=pltpu.CompilerParams(vmem_limit_bytes=vmem),
        cost_estimate=pl.CostEstimate(flops=flops, bytes_accessed=1 << 20, transcendentals=0),
    )(*args)
    return list(results)


def exchange(faces):
    out = []
    for axis, (low, high) in zip(AXES, zip(faces[::2], faces[1::2])):
        n = lax.axis_size(axis)
        up = [(i, i + 1) for i in range(n - 1)]
        down = [(j, i) for i, j in up]
        out.append(lax.ppermute(high, axis, up))
        out.append(lax.ppermute(low, axis, down))
    return out


def sum_over(x, axis):
    n = lax.axis_size(axis)
    if n & (n - 1):
        return lax.psum(x, axis)
    if n <= 4:
        parts = [lax.ppermute(x, axis, [(i, i ^ s) for i in range(n)]) for s in range(1, n)]
        return functools.reduce(jnp.add, parts, x)
    step = 1
    while step < n:
        x = x + lax.ppermute(x, axis, [(i, i ^ step) for i in range(n)])
        step *= 2
    return x


def total(x):
    n = lax.axis_size("gy")
    if n != 2:
        return sum_over(sum_over(sum_over(x, "gy"), "gx"), "gz")
    half = x.shape[0] // 2
    me = lax.axis_index("gy")
    swap = [(0, 1), (1, 0)]
    piece = lambda k: lax.dynamic_slice_in_dim(x, k * half, half, 0)
    mine = piece(me) + lax.ppermute(piece(1 - me), "gy", swap)
    mine = sum_over(sum_over(mine, "gx"), "gz")
    theirs = lax.ppermute(mine, "gy", swap)
    return jnp.where(me == 0, jnp.concatenate([mine, theirs], 0), jnp.concatenate([theirs, mine], 0))


def local(start_block, stiff_field, shift_field, mass_field):
    gd = Grid(start_block.shape)
    v, nz, lanes = gd.v, gd.nz, gd.lanes
    nodes = stiff_field.size
    count = nodes * gd.c
    for axis in AXES:
        count *= lax.axis_size(axis)
    scale = 1.0 / count
    rows = gd.nx * gd.ny
    fields = [f.reshape(rows, nz) for f in (stiff_field, shift_field, mass_field)]
    first_faces = [(v, gd.xface + nz)] * 2 + [(v, gd.yface + nz)] * 2 + [(v + 8, nz)] * 2
    faces = [(v, gd.xface)] * 2 + [(v, gd.yface)] * 2 + [(v, nz)] * 2
    full = (v, lanes)

    packed = call(functools.partial(pack_kernel, gd), [full, (8, rows * nz)] + first_faces,
                  [start_block.reshape(v * gd.blocks, nz)] + fields)
    sm, coef = packed[:2]
    halo_s = exchange(packed[2:])
    gram_scratch = lambda n: [((2 * v, lanes), BF16), ((n * v, lanes), BF16), ((n * v, lanes), BF16)]
    imaged = call(functools.partial(image_kernel, gd), [full, (v, 2 * v)] + faces,
                  [sm, coef] + halo_s, gram_scratch(2), flops=1 << 28)
    ks, gram0 = imaged[:2]
    halo_u = exchange(imaged[2:])
    coef0, theta0 = call(functools.partial(dense0_kernel, scale), [(v, 2 * v), (v, v)], [total(gram0)])

    res = call(functools.partial(residual_kernel, gd, False, 1),
               [full, full, (v, 4 * v)] + faces + faces,
               [coef0, coef, ks, sm] + halo_u + halo_s,
               [((2 * v, 2 * v), BF16)] + gram_scratch(4), flops=1 << 29)
    r0, kr0, gram1 = res[:3]
    halo_r, halo_b = res[3:9], exchange(res[9:])
    gram1 = total(gram1)
    coef1, theta1 = call(functools.partial(dense1_kernel, scale), [(v, 4 * v), (v, v)], [gram1, coef0, theta0])

    res = call(functools.partial(residual_kernel, gd, True, 2),
               [full, (v, 6 * v)] + faces,
               [coef1, coef, ks, kr0, sm, r0] + halo_u + halo_b + halo_s + halo_r,
               [((2 * v, 4 * v), BF16)] + gram_scratch(6), flops=1 << 29, vmem=56 << 20)
    r1, gram2 = res[:2]
    (prev,) = call(functools.partial(previous_kernel, scale), [(v, 4 * v)], [gram1, coef1])
    coef2, theta2 = call(functools.partial(dense2_kernel, scale), [(v, 4 * v), (v, v)],
                         [total(gram2), prev, coef1, theta1])
    (modes,) = call(functools.partial(final_kernel, gd), [(v * gd.blocks, nz)],
                    [coef2, sm, r0, r1], [((2 * v, 4 * v), BF16)])
    return modes.reshape(start_block.shape), theta2


def solution(mesh):
    grid = P("gx", "gy", "gz")
    block = P(None, None, "gx", "gy", "gz")
    return jax.shard_map(local, mesh=mesh, in_specs=(block, grid, grid, grid),
                         out_specs=(block, P()), check_vma=False)
```

time: 752 us -> 254 us (0.34)
  waiting for transfers between devices: 318 us -> 105 us
  other arithmetic: 146 us -> 3.05 us
  local copies, waits for them, and re-layouts: 95.4 us -> 21.1 us
  matrix products: 61.6 us -> 0 us
  Pallas kernels: 0 us -> 56.2 us
  blocking collectives: 40.4 us -> 0 us
  between operations: 16.8 us -> 1.22 us
    psum x2 -> x0, waiting for transfers between devices: 266 us -> none  [local(): lax.psum((gram_of(search_set, image_set), gram_of(search_set, mass_field...]
    another operation x34 -> x0, other arithmetic: 109 us -> none  [the longest x10 41.2 us: ritz_filter(): factor = jnp.linalg.cholesky(pencil_m)]
    pallas_call x0 -> x9, Pallas kernels: none -> 56.2 us  [call(): pl.pallas_call(kernel, out_shape=[jax.ShapeDtypeStruct(s, F32) for s in o...]
    ppermute x24 -> x42, waiting for transfers between devices: 51.8 us -> 105 us  [the longest x18 72 us: sum_over(): lax.ppermute(x, axis, [(i, i ^ s) for i in range(n)])]
    dot_general x27 -> x0, matrix products: 51.1 us -> none  [hidot(): jnp.dot(left, right, precision=lax.Precision.HIGHEST, preferred_element_t...]
    psum x1 -> x0, blocking collectives: 40.4 us -> none  [start_sums(): lax.psum((gram_of(start_block, mass_field * start_block), gram_of(start_b...]
    slice x15 -> x0, local copies, waits for them, and re-layouts: 37.2 us -> none  [the longest x7 24.8 us: with_halo(): initial = lax.slice_in_dim(x, 0, width, axis=dim)]
    ppermute x6 -> x0, local copies, waits for them, and re-layouts: 20.3 us -> none  [the longest x3 10.2 us: with_halo(): after = lax.ppermute(initial, axis, down)]
  transfers between devices with their start and end apart: 26 -> 42, of which waited for: 9 -> 22; matrix products, arithmetic and copies ran while one was open for 10% -> 1% of each run, Pallas kernels for 0% -> 4%
where the time goes in v1:
time: 254 us; the launch traced here: 253 us
  waiting for transfers between devices  105 us (41%)
  starting transfers between devices  66.9 us (26%)
  Pallas kernels  56.2 us (22%)
  local copies, waits for them, and re-layouts  21.1 us (8%)
  other arithmetic  3.05 us (1%)
    ppermute x18, waiting for transfers between devices, sum_over(): lax.ppermute(x, axis, [(i, i ^ s) for i in range(n)])  72 us
    pallas_call x9, Pallas kernels, call(): pl.pallas_call(kernel, out_shape=[jax.ShapeDtypeStruct(s, F32) for s in o...  56.2 us
    ppermute x18, starting transfers between devices, sum_over(): lax.ppermute(x, axis, [(i, i ^ s) for i in range(n)])  30.1 us
    ppermute x9, waiting for transfers between devices, exchange(): out.append(lax.ppermute(low, axis, down))  25.9 us
    ppermute x9, starting transfers between devices, exchange(): out.append(lax.ppermute(high, axis, up))  21.6 us
    unnamed x86, local copies, waits for them, and re-layouts  19.6 us
    ppermute x9, starting transfers between devices, exchange(): out.append(lax.ppermute(low, axis, down))  11.8 us
  transfers between devices with their start and end apart: 42, of which 22 were waited for; matrix products, arithmetic and copies ran while one was open for 1% of the time, Pallas kernels for 4%

profile of v1, /device:TPU:0, one launch (start us, length us, event | category | flops | bytes accessed | tf_op | source)
XLA Modules:
  0.0 253.0 jit_solution(14907230450336847210)
XLA Ops:
  4.1 2.3 shard_map.59
  6.5 4.9 %collective-permute-start = (f32[64,3200]{1,0:T(8,128)}, f32[64,3200]{1,0:T(8,128)S(1)}, u32[]{:S(2)}, u32[]{:S(2)}) collective-permute-start(f32[64,3200]{1,0:T(8,128)} %get-tuple-element.43), channel_id=1, source_target_pairs={{0,8},{8,16},{16,24},{1,9},{9,17},{17,25},{2,10},{10,18},{18,26},{... | collective-permute-start | bytes 2457608 | tf_op jit(solution)/shard_map/ppermute | solution.py:418
  15.5 3.5 %collective-permute-start.4 = (f32[72,128]{1,0:T(8,128)S(1)}, f32[72,128]{1,0:T(8,128)S(1)}, u32[]{:S(2)}, u32[]{:S(2)}) collective-permute-start(f32[72,128]{1,0:T(8,128)S(1)} %get-tuple-element.47), channel_id=1, source_target_pairs={{0,1},{1,2},{2,3},{4,5},{5,6},{6,7},{8,9},{9,10},{10,11},{12,13},{... | collective-permute-start | bytes 110600 | tf_op jit(solution)/shard_map/ppermute | solution.py:418
  21.9 5.5 %collective-permute-done.5.za.refs_15_.refs_23_ = f32[72,128]{1,0:T(8,128)} collective-permute-done((f32[72,128]{1,0:T(8,128)}, f32[72,128]{1,0:T(8,128)}, u32[]{:S(2)}, u32[]{:S(2)}) %collective-permute-start.5) | collective-permute-done | bytes 36896 | tf_op jit(solution)/shard_map/ppermute | solution.py:419
  27.4 1.7 collective-permute-done.xb.refs_10_.refs_18_
  29.1 19.4 %collective-permute-done.1.xa.refs_11_.refs_19_ = f32[64,3200]{1,0:T(8,128)S(1)} collective-permute-done((f32[64,3200]{1,0:T(8,128)}, f32[64,3200]{1,0:T(8,128)S(1)}, u32[]{:S(2)}, u32[]{:S(2)}) %collective-permute-start.1) | collective-permute-done | bytes 819232 | tf_op jit(solution)/shard_map/ppermute | solution.py:419
  48.5 5.3 %shard_map.60 = (f32[64,6144]{1,0:T(8,128)S(1)}, f32[64,128]{1,0:T(8,128)S(1)}, f32[64,3072]{1,0:T(8,128)S(1)}, f32[64,3072]{1,0:T(8,128)S(1)}, f32[64,768]{1,0:...) custom-call(f32[64,6144]{1,0:T(8,128)S(1)} %get-tuple-element.41.sm_ref.refs_3_.refs_4_.s_ref, ...), custom_call_target="tpu_custom_call" | custom-call | flops 268435456 | bytes 1048576 | tf_op jit(solution)/shard_map/pallas_call | solution.py:400
  60.0 3.4 %collective-permute-start.14 = (f32[64,3072]{1,0:T(8,128)}, f32[64,3072]{1,0:T(8,128)S(1)}, u32[]{:S(2)}, u32[]{:S(2)}) collective-permute-start(f32[64,3072]{1,0:T(8,128)} %copy-done.32), channel_id=1, source_target_pairs={{0,8},{8,16},{16,24},{1,9},{9,17},{17,25},{2,10},{10,18},{18,26},{... | collective-permute-start | bytes 2359304 | tf_op jit(solution)/shard_map/ppermute | solution.py:418
  65.8 3.8 %collective-permute-start.8 = (f32[32,128]{1,0:T(8,128)S(1)}, f32[32,128]{1,0:T(8,128)S(1)}, u32[]{:S(2)}, u32[]{:S(2)}) collective-permute-start(f32[32,128]{1,0:T(8,128)S(1)} %dynamic-slice_add_fusion.2), channel_id=1, source_target_pairs={{0,16},{8,24},{16,0},{24,8},{1,17},{9,25},{17,1},{25,9},{2,18},{10... | collective-permute-start | bytes 49160 | tf_op jit(solution)/shard_map/ppermute | solution.py:428
  69.6 14.0 %collective-permute-done.9 = f32[32,128]{1,0:T(8,128)S(1)} collective-permute-done((f32[32,128]{1,0:T(8,128)S(1)}, f32[32,128]{1,0:T(8,128)S(1)}, u32[]{:S(2)}, u32[]{:S(2)}) %collective-permute-start.9) | collective-permute-done | bytes 16416 | tf_op jit(solution)/shard_map/ppermute | solution.py:428
  83.6 15.8 %collective-permute-done.7 = f32[32,128]{1,0:T(8,128)S(1)} collective-permute-done((f32[32,128]{1,0:T(8,128)S(1)}, f32[32,128]{1,0:T(8,128)S(1)}, u32[]{:S(2)}, u32[]{:S(2)}) %collective-permute-start.7) | collective-permute-done | bytes 16416 | tf_op jit(solution)/shard_map/ppermute | solution.py:428
  99.4 3.6 %collective-permute-start.12 = (f32[32,128]{1,0:T(8,128)S(1)}, f32[32,128]{1,0:T(8,128)S(1)}, u32[]{:S(2)}, u32[]{:S(2)}) collective-permute-start(f32[32,128]{1,0:T(8,128)S(1)} %add_add_fusion.5), channel_id=1, source_target_pairs={{0,3},{1,2},{2,1},{3,0},{4,7},{5,6},{6,5},{7,4},{8,11},{9,10},{10,... | collective-permute-start | bytes 49160 | tf_op jit(solution)/shard_map/ppermute | solution.py:428
  105.0 1.9 collective-permute-start.18
  107.7 2.0 collective-permute-start.16
  112.1 1.8 collective-permute-start.13
  117.4 2.7 %shard_map.61 = (f32[64,128]{1,0:T(8,128)S(1)}, f32[64,64]{1,0:T(8,128)S(1)}) custom-call(f32[64,128]{1,0:T(8,128)S(1)} %maximum_select_fusion.2.gram_ref), custom_call_target="tpu_custom_call" | custom-call | flops 1048576 | bytes 1048576 | tf_op jit(solution)/shard_map/pallas_call | solution.py:400
  121.2 1.9 copy-done.5
  123.9 9.1 %shard_map.62 = (f32[64,6144]{1,0:T(8,128)S(1)}, f32[64,6144]{1,0:T(8,128)S(1)}, f32[64,256]{1,0:T(8,128)S(1)}, f32[64,3072]{1,0:T(8,128)S(1)}, f32[64,3072]{1,0...) custom-call(f32[64,128]{1,0:T(8,128)S(1)} %get-tuple-element.50.refs, ...), custom_call_target="tpu_custom_call" | custom-call | flops 536870912 | bytes 1048576 | tf_op jit(solution)/shard_map/pallas_call | solution.py:400
  140.0 4.0 %collective-permute-start.23 = (f32[32,256]{1,0:T(8,128)S(1)}, f32[32,256]{1,0:T(8,128)S(1)}, u32[]{:S(2)}, u32[]{:S(2)}) collective-permute-start(f32[32,256]{1,0:T(8,128)S(1)} %dynamic-slice_add_fusion.1), channel_id=1, source_target_pairs={{0,24},{8,16},{16,8},{24,0},{1,25},{9,17},{17,9},{25,1},{2,26},{10... | collective-permute-start | bytes 98312 | tf_op jit(solution)/shard_map/ppermute | solution.py:428
  146.8 15.9 %collective-permute-done.23 = f32[32,256]{1,0:T(8,128)S(1)} collective-permute-done((f32[32,256]{1,0:T(8,128)S(1)}, f32[32,256]{1,0:T(8,128)S(1)}, u32[]{:S(2)}, u32[]{:S(2)}) %collective-permute-start.23) | collective-permute-done | bytes 32800 | tf_op jit(solution)/shard_map/ppermute | solution.py:428
  162.8 15.3 %collective-permute-done.21 = f32[32,256]{1,0:T(8,128)S(1)} collective-permute-done((f32[32,256]{1,0:T(8,128)S(1)}, f32[32,256]{1,0:T(8,128)S(1)}, u32[]{:S(2)}, u32[]{:S(2)}) %collective-permute-start.21) | collective-permute-done | bytes 32800 | tf_op jit(solution)/shard_map/ppermute | solution.py:428
  178.1 4.6 %collective-permute-start.26 = (f32[32,256]{1,0:T(8,128)S(1)}, f32[32,256]{1,0:T(8,128)S(1)}, u32[]{:S(2)}, u32[]{:S(2)}) collective-permute-start(f32[32,256]{1,0:T(8,128)S(1)} %add_add_fusion.3), channel_id=1, source_target_pairs={{0,3},{1,2},{2,1},{3,0},{4,7},{5,6},{6,5},{7,4},{8,11},{9,10},{10,... | collective-permute-start | bytes 98312 | tf_op jit(solution)/shard_map/ppermute | solution.py:428
  184.9 1.7 collective-permute-start.32
  193.5 7.3 %shard_map.63 = (f32[64,256]{1,0:T(8,128)S(1)}, f32[64,64]{1,0:T(8,128)S(1)}) custom-call(f32[64,256]{1,0:T(8,128)S(1)} %maximum_select_fusion.1.gram_ref, f32[64,128]{1,0:T(8,128)S(1)} %get-tuple-element.50.refs_0_.coef_ref, f32[64,64]{1,0:T(8,128)S(1)} %get-tuple-element.59.theta_ref), custom_call_target="tpu_custom_call" | custom-call | flops 1048576 | bytes 1048576 | tf_op jit(solution)/shard_map/pallas_call | solution.py:400
  202.7 15.4 %shard_map.64 = (f32[64,6144]{1,0:T(8,128)}, f32[64,384]{1,0:T(8,128)}, f32[64,3072]{1,0:T(8,128)}, f32[64,3072]{1,0:T(8,128)}, f32[64,768]{1,0:T(8,128)}, /*ind...) custom-call(f32[64,256]{1,0:T(8,128)} %copy-done.17, f32[8,2048]{1,0:T(8,128)} %copy-done.16, ...), custom_call_target="tpu_custom_call" | custom-call | flops 536870912 | bytes 1048576 | tf_op jit(solution)/shard_map/pallas_call | solution.py:400
  222.3 2.2 collective-permute-start.35
  224.5 1.8 collective-permute-done.37
  226.7 5.4 %collective-permute-start.40 = (f32[32,384]{1,0:T(8,128)S(1)}, f32[32,384]{1,0:T(8,128)S(1)}, u32[]{:S(2)}, u32[]{:S(2)}) collective-permute-start(f32[32,384]{1,0:T(8,128)S(1)} %add_add_fusion.1), channel_id=1, source_target_pairs={{0,3},{1,2},{2,1},{3,0},{4,7},{5,6},{6,5},{7,4},{8,11},{9,10},{10,... | collective-permute-start | bytes 147464 | tf_op jit(solution)/shard_map/ppermute | solution.py:428
  232.8 2.0 collective-permute-done.40
  234.8 2.3 collective-permute-done.39
  238.5 10.6 %shard_map.66 = (f32[64,256]{1,0:T(8,128)S(1)}, f32[64,64]{1,0:T(8,128)}) custom-call(f32[64,384]{1,0:T(8,128)S(1)} %maximum_select_fusion.gram_ref, f32[64,256]{1,0:T(8,128)S(1)} %shard_map.65.prev_ref, f32[64,256]{1,0:T(8,128)S(1)} %copy-done.18, f32[64,64]{1,0:T(8,128)S(1)} %get-tuple-element.76.theta1_ref), custom_call_target="tpu_custom_call" | custom-call | flops 1048576 | bytes 1048576 | tf_op jit(solution)/shard_map/pallas_call | solution.py:400
  250.5 2.5 shard_map.67
  (162 shorter events, 58.0 us)
Async XLA Ops:
  6.5 22.7 %collective-permute-start = (f32[64,3200]{1,0:T(8,128)}, f32[64,3200]{1,0:T(8,128)S(1)}, u32[]{:S(2)}, u32[]{:S(2)}) collective-permute-start(f32[64,3200]{1,0:T(8,128)} %get-tuple-element.43), channel_id=1, source_target_pairs={{0,8},{8,16},{16,24},{1,9},{9,17},{17,25},{2,10},{10,18},{18,26},{... | collective-permute-start | bytes 2457608 | tf_op jit(solution)/shard_map/ppermute | solution.py:418
  11.4 37.1 %collective-permute-start.1 = (f32[64,3200]{1,0:T(8,128)}, f32[64,3200]{1,0:T(8,128)S(1)}, u32[]{:S(2)}, u32[]{:S(2)}) collective-permute-start(f32[64,3200]{1,0:T(8,128)} %get-tuple-element.44), channel_id=1, source_target_pairs={{8,0},{16,8},{24,16},{9,1},{17,9},{25,17},{10,2},{18,10},{26,18},{... | collective-permute-start | bytes 2457608 | tf_op jit(solution)/shard_map/ppermute | solution.py:419
  12.7 14.7 %collective-permute-start.2 = (f32[64,896]{1,0:T(8,128)}, f32[64,896]{1,0:T(8,128)S(1)}, u32[]{:S(2)}, u32[]{:S(2)}) collective-permute-start(f32[64,896]{1,0:T(8,128)} %get-tuple-element.45), channel_id=1, source_target_pairs={{0,4},{1,5},{2,6},{3,7},{8,12},{9,13},{10,14},{11,15},{16,20},{17,... | collective-permute-start | bytes 688136 | tf_op jit(solution)/shard_map/ppermute | solution.py:418
  14.2 13.2 %collective-permute-start.3 = (f32[64,896]{1,0:T(8,128)}, f32[64,896]{1,0:T(8,128)}, u32[]{:S(2)}, u32[]{:S(2)}) collective-permute-start(f32[64,896]{1,0:T(8,128)} %get-tuple-element.46), channel_id=1, source_target_pairs={{4,0},{5,1},{6,2},{7,3},{12,8},{13,9},{14,10},{15,11},{20,16},{21,... | collective-permute-start | bytes 688136 | tf_op jit(solution)/shard_map/ppermute | solution.py:419
  15.5 5.1 %collective-permute-start.4 = (f32[72,128]{1,0:T(8,128)S(1)}, f32[72,128]{1,0:T(8,128)S(1)}, u32[]{:S(2)}, u32[]{:S(2)}) collective-permute-start(f32[72,128]{1,0:T(8,128)S(1)} %get-tuple-element.47), channel_id=1, source_target_pairs={{0,1},{1,2},{2,3},{4,5},{5,6},{6,7},{8,9},{9,10},{10,11},{12,13},{... | collective-permute-start | bytes 110600 | tf_op jit(solution)/shard_map/ppermute | solution.py:418
  20.6 6.8 %collective-permute-start.5 = (f32[72,128]{1,0:T(8,128)}, f32[72,128]{1,0:T(8,128)}, u32[]{:S(2)}, u32[]{:S(2)}) collective-permute-start(f32[72,128]{1,0:T(8,128)} %get-tuple-element.48), channel_id=1, source_target_pairs={{1,0},{2,1},{3,2},{5,4},{6,5},{7,6},{9,8},{10,9},{11,10},{13,12},{... | collective-permute-start | bytes 110600 | tf_op jit(solution)/shard_map/ppermute | solution.py:419
  60.0 61.1 %collective-permute-start.14 = (f32[64,3072]{1,0:T(8,128)}, f32[64,3072]{1,0:T(8,128)S(1)}, u32[]{:S(2)}, u32[]{:S(2)}) collective-permute-start(f32[64,3072]{1,0:T(8,128)} %copy-done.32), channel_id=1, source_target_pairs={{0,8},{8,16},{16,24},{1,9},{9,17},{17,25},{2,10},{10,18},{18,26},{... | collective-permute-start | bytes 2359304 | tf_op jit(solution)/shard_map/ppermute | solution.py:418
  63.4 57.7 %collective-permute-start.15 = (f32[64,3072]{1,0:T(8,128)}, f32[64,3072]{1,0:T(8,128)S(1)}, u32[]{:S(2)}, u32[]{:S(2)}) collective-permute-start(f32[64,3072]{1,0:T(8,128)} %copy-done.31), channel_id=1, source_target_pairs={{8,0},{16,8},{24,16},{9,1},{17,9},{25,17},{10,2},{18,10},{26,18},{... | collective-permute-start | bytes 2359304 | tf_op jit(solution)/shard_map/ppermute | solution.py:419
  65.5 18.1 %collective-permute-start.9 = (f32[32,128]{1,0:T(8,128)S(1)}, f32[32,128]{1,0:T(8,128)S(1)}, u32[]{:S(2)}, u32[]{:S(2)}) collective-permute-start(f32[32,128]{1,0:T(8,128)S(1)} %dynamic-slice_add_fusion.2), channel_id=1, source_target_pairs={{0,24},{8,16},{16,8},{24,0},{1,25},{9,17},{17,9},{25,1},{2,26},{10... | collective-permute-start | bytes 49160 | tf_op jit(solution)/shard_map/ppermute | solution.py:428
  65.8 17.8 %collective-permute-start.8 = (f32[32,128]{1,0:T(8,128)S(1)}, f32[32,128]{1,0:T(8,128)S(1)}, u32[]{:S(2)}, u32[]{:S(2)}) collective-permute-start(f32[32,128]{1,0:T(8,128)S(1)} %dynamic-slice_add_fusion.2), channel_id=1, source_target_pairs={{0,16},{8,24},{16,0},{24,8},{1,17},{9,25},{17,1},{25,9},{2,18},{10... | collective-permute-start | bytes 49160 | tf_op jit(solution)/shard_map/ppermute | solution.py:428
  69.6 29.8 %collective-permute-start.7 = (f32[32,128]{1,0:T(8,128)S(1)}, f32[32,128]{1,0:T(8,128)S(1)}, u32[]{:S(2)}, u32[]{:S(2)}) collective-permute-start(f32[32,128]{1,0:T(8,128)S(1)} %dynamic-slice_add_fusion.2), channel_id=1, source_target_pairs={{0,8},{8,0},{16,24},{24,16},{1,9},{9,1},{17,25},{25,17},{2,10},{10... | collective-permute-start | bytes 49160 | tf_op jit(solution)/shard_map/ppermute | solution.py:428
  99.4 5.6 %collective-permute-start.12 = (f32[32,128]{1,0:T(8,128)S(1)}, f32[32,128]{1,0:T(8,128)S(1)}, u32[]{:S(2)}, u32[]{:S(2)}) collective-permute-start(f32[32,128]{1,0:T(8,128)S(1)} %add_add_fusion.5), channel_id=1, source_target_pairs={{0,3},{1,2},{2,1},{3,0},{4,7},{5,6},{6,5},{7,4},{8,11},{9,10},{10,... | collective-permute-start | bytes 49160 | tf_op jit(solution)/shard_map/ppermute | solution.py:428
  103.0 6.6 %collective-permute-start.10 = (f32[32,128]{1,0:T(8,128)S(1)}, f32[32,128]{1,0:T(8,128)S(1)}, u32[]{:S(2)}, u32[]{:S(2)}) collective-permute-start(f32[32,128]{1,0:T(8,128)S(1)} %add_add_fusion.5), channel_id=1, source_target_pairs={{0,1},{1,0},{2,3},{3,2},{4,5},{5,4},{6,7},{7,6},{8,9},{9,8},{10,11... | collective-permute-start | bytes 49160 | tf_op jit(solution)/shard_map/ppermute | solution.py:428
  105.0 6.5 %collective-permute-start.18 = (f32[64,128]{1,0:T(8,128)}, f32[64,128]{1,0:T(8,128)S(1)}, u32[]{:S(2)}, u32[]{:S(2)}) collective-permute-start(f32[64,128]{1,0:T(8,128)} %copy-done.36), channel_id=1, source_target_pairs={{0,1},{1,2},{2,3},{4,5},{5,6},{6,7},{8,9},{9,10},{10,11},{12,13},{... | collective-permute-start | bytes 98312 | tf_op jit(solution)/shard_map/ppermute | solution.py:418
  107.7 13.5 %collective-permute-start.16 = (f32[64,768]{1,0:T(8,128)}, f32[64,768]{1,0:T(8,128)}, u32[]{:S(2)}, u32[]{:S(2)}) collective-permute-start(f32[64,768]{1,0:T(8,128)} %copy-done.34), channel_id=1, source_target_pairs={{0,4},{1,5},{2,6},{3,7},{8,12},{9,13},{10,14},{11,15},{16,20},{17,... | collective-permute-start | bytes 589832 | tf_op jit(solution)/shard_map/ppermute | solution.py:418
  109.6 11.5 %collective-permute-start.17 = (f32[64,768]{1,0:T(8,128)}, f32[64,768]{1,0:T(8,128)}, u32[]{:S(2)}, u32[]{:S(2)}) collective-permute-start(f32[64,768]{1,0:T(8,128)} %copy-done.33), channel_id=1, source_target_pairs={{4,0},{5,1},{6,2},{7,3},{12,8},{13,9},{14,10},{15,11},{20,16},{21,... | collective-permute-start | bytes 589832 | tf_op jit(solution)/shard_map/ppermute | solution.py:419
  115.1 6.0 %collective-permute-start.19 = (f32[64,128]{1,0:T(8,128)}, f32[64,128]{1,0:T(8,128)S(1)}, u32[]{:S(2)}, u32[]{:S(2)}) collective-permute-start(f32[64,128]{1,0:T(8,128)} %copy-done.35), channel_id=1, source_target_pairs={{1,0},{2,1},{3,2},{5,4},{6,5},{7,6},{9,8},{10,9},{11,10},{13,12},{... | collective-permute-start | bytes 98312 | tf_op jit(solution)/shard_map/ppermute | solution.py:419
  137.1 64.3 %collective-permute-start.28 = (f32[64,3072]{1,0:T(8,128)S(1)}, f32[64,3072]{1,0:T(8,128)S(1)}, u32[]{:S(2)}, u32[]{:S(2)}) collective-permute-start(f32[64,3072]{1,0:T(8,128)S(1)} %get-tuple-element.63), channel_id=1, source_target_pairs={{0,8},{8,16},{16,24},{1,9},{9,17},{17,25},{2,10},{10,18},{18,26},{... | collective-permute-start | bytes 2359304 | tf_op jit(solution)/shard_map/ppermute | solution.py:418
  138.7 62.8 %collective-permute-start.29 = (f32[64,3072]{1,0:T(8,128)S(1)}, f32[64,3072]{1,0:T(8,128)S(1)}, u32[]{:S(2)}, u32[]{:S(2)}) collective-permute-start(f32[64,3072]{1,0:T(8,128)S(1)} %get-tuple-element.64), channel_id=1, source_target_pairs={{8,0},{16,8},{24,16},{9,1},{17,9},{25,17},{10,2},{18,10},{26,18},{... | collective-permute-start | bytes 2359304 | tf_op jit(solution)/shard_map/ppermute | solution.py:419
  140.0 22.8 %collective-permute-start.23 = (f32[32,256]{1,0:T(8,128)S(1)}, f32[32,256]{1,0:T(8,128)S(1)}, u32[]{:S(2)}, u32[]{:S(2)}) collective-permute-start(f32[32,256]{1,0:T(8,128)S(1)} %dynamic-slice_add_fusion.1), channel_id=1, source_target_pairs={{0,24},{8,16},{16,8},{24,0},{1,25},{9,17},{17,9},{25,1},{2,26},{10... | collective-permute-start | bytes 98312 | tf_op jit(solution)/shard_map/ppermute | solution.py:428
  144.0 18.8 %collective-permute-start.22 = (f32[32,256]{1,0:T(8,128)S(1)}, f32[32,256]{1,0:T(8,128)S(1)}, u32[]{:S(2)}, u32[]{:S(2)}) collective-permute-start(f32[32,256]{1,0:T(8,128)S(1)} %dynamic-slice_add_fusion.1), channel_id=1, source_target_pairs={{0,16},{8,24},{16,0},{24,8},{1,17},{9,25},{17,1},{25,9},{2,18},{10... | collective-permute-start | bytes 98312 | tf_op jit(solution)/shard_map/ppermute | solution.py:428
  145.4 32.6 %collective-permute-start.21 = (f32[32,256]{1,0:T(8,128)S(1)}, f32[32,256]{1,0:T(8,128)S(1)}, u32[]{:S(2)}, u32[]{:S(2)}) collective-permute-start(f32[32,256]{1,0:T(8,128)S(1)} %dynamic-slice_add_fusion.1), channel_id=1, source_target_pairs={{0,8},{8,0},{16,24},{24,16},{1,9},{9,1},{17,25},{25,17},{2,10},{10... | collective-permute-start | bytes 98312 | tf_op jit(solution)/shard_map/ppermute | solution.py:428
  178.1 6.8 %collective-permute-start.26 = (f32[32,256]{1,0:T(8,128)S(1)}, f32[32,256]{1,0:T(8,128)S(1)}, u32[]{:S(2)}, u32[]{:S(2)}) collective-permute-start(f32[32,256]{1,0:T(8,128)S(1)} %add_add_fusion.3), channel_id=1, source_target_pairs={{0,3},{1,2},{2,1},{3,0},{4,7},{5,6},{6,5},{7,4},{8,11},{9,10},{10,... | collective-permute-start | bytes 98312 | tf_op jit(solution)/shard_map/ppermute | solution.py:428
  182.7 6.1 %collective-permute-start.24 = (f32[32,256]{1,0:T(8,128)S(1)}, f32[32,256]{1,0:T(8,128)S(1)}, u32[]{:S(2)}, u32[]{:S(2)}) collective-permute-start(f32[32,256]{1,0:T(8,128)S(1)} %add_add_fusion.3), channel_id=1, source_target_pairs={{0,1},{1,0},{2,3},{3,2},{4,5},{5,4},{6,7},{7,6},{8,9},{9,8},{10,11... | collective-permute-start | bytes 98312 | tf_op jit(solution)/shard_map/ppermute | solution.py:428
  184.9 5.2 %collective-permute-start.32 = (f32[64,128]{1,0:T(8,128)S(1)}, f32[64,128]{1,0:T(8,128)S(1)}, u32[]{:S(2)}, u32[]{:S(2)}) collective-permute-start(f32[64,128]{1,0:T(8,128)S(1)} %get-tuple-element.67), channel_id=1, source_target_pairs={{0,1},{1,2},{2,3},{4,5},{5,6},{6,7},{8,9},{9,10},{10,11},{12,13},{... | collective-permute-start | bytes 98312 | tf_op jit(solution)/shard_map/ppermute | solution.py:418
  187.5 13.9 %collective-permute-start.30 = (f32[64,768]{1,0:T(8,128)S(1)}, f32[64,768]{1,0:T(8,128)S(1)}, u32[]{:S(2)}, u32[]{:S(2)}) collective-permute-start(f32[64,768]{1,0:T(8,128)S(1)} %get-tuple-element.65), channel_id=1, source_target_pairs={{0,4},{1,5},{2,6},{3,7},{8,12},{9,13},{10,14},{11,15},{16,20},{17,... | collective-permute-start | bytes 589832 | tf_op jit(solution)/shard_map/ppermute | solution.py:418
  188.8 12.6 %collective-permute-start.31 = (f32[64,768]{1,0:T(8,128)S(1)}, f32[64,768]{1,0:T(8,128)S(1)}, u32[]{:S(2)}, u32[]{:S(2)}) collective-permute-start(f32[64,768]{1,0:T(8,128)S(1)} %get-tuple-element.66), channel_id=1, source_target_pairs={{4,0},{5,1},{6,2},{7,3},{12,8},{13,9},{14,10},{15,11},{20,16},{21,... | collective-permute-start | bytes 589832 | tf_op jit(solution)/shard_map/ppermute | solution.py:419
  192.2 9.2 %collective-permute-start.33 = (f32[64,128]{1,0:T(8,128)S(1)}, f32[64,128]{1,0:T(8,128)S(1)}, u32[]{:S(2)}, u32[]{:S(2)}) collective-permute-start(f32[64,128]{1,0:T(8,128)S(1)} %get-tuple-element.68), channel_id=1, source_target_pairs={{1,0},{2,1},{3,2},{5,4},{6,5},{7,6},{9,8},{10,9},{11,10},{13,12},{... | collective-permute-start | bytes 98312 | tf_op jit(solution)/shard_map/ppermute | solution.py:419
  221.0 5.3 %collective-permute-start.37 = (f32[32,384]{1,0:T(8,128)S(1)}, f32[32,384]{1,0:T(8,128)S(1)}, u32[]{:S(2)}, u32[]{:S(2)}) collective-permute-start(f32[32,384]{1,0:T(8,128)S(1)} %dynamic-slice_add_fusion), channel_id=1, source_target_pairs={{0,24},{8,16},{16,8},{24,0},{1,25},{9,17},{17,9},{25,1},{2,26},{10... | collective-permute-start | bytes 147464 | tf_op jit(solution)/shard_map/ppermute | solution.py:428
  221.3 5.1 %collective-permute-start.36 = (f32[32,384]{1,0:T(8,128)S(1)}, f32[32,384]{1,0:T(8,128)S(1)}, u32[]{:S(2)}, u32[]{:S(2)}) collective-permute-start(f32[32,384]{1,0:T(8,128)S(1)} %dynamic-slice_add_fusion), channel_id=1, source_target_pairs={{0,16},{8,24},{16,0},{24,8},{1,17},{9,25},{17,1},{25,9},{2,18},{10... | collective-permute-start | bytes 147464 | tf_op jit(solution)/shard_map/ppermute | solution.py:428
  226.7 8.0 %collective-permute-start.40 = (f32[32,384]{1,0:T(8,128)S(1)}, f32[32,384]{1,0:T(8,128)S(1)}, u32[]{:S(2)}, u32[]{:S(2)}) collective-permute-start(f32[32,384]{1,0:T(8,128)S(1)} %add_add_fusion.1), channel_id=1, source_target_pairs={{0,3},{1,2},{2,1},{3,0},{4,7},{5,6},{6,5},{7,4},{8,11},{9,10},{10,... | collective-permute-start | bytes 147464 | tf_op jit(solution)/shard_map/ppermute | solution.py:428
  232.1 5.0 %collective-permute-start.39 = (f32[32,384]{1,0:T(8,128)S(1)}, f32[32,384]{1,0:T(8,128)S(1)}, u32[]{:S(2)}, u32[]{:S(2)}) collective-permute-start(f32[32,384]{1,0:T(8,128)S(1)} %add_add_fusion.1), channel_id=1, source_target_pairs={{0,2},{1,3},{2,0},{3,1},{4,6},{5,7},{6,4},{7,5},{8,10},{9,11},{10,... | collective-permute-start | bytes 147464 | tf_op jit(solution)/shard_map/ppermute | solution.py:428
  (53 other events, 1011.0 us)

commit v2 on v1

v2 whole, which is shorter than its diff:
```python
import functools

import jax
import jax.numpy as jnp
from jax import lax
from jax.experimental import pallas as pl
from jax.experimental.pallas import tpu as pltpu
from jax.sharding import PartitionSpec as P


FILTER = 4
AXES = ("gx", "gy", "gz")
F32 = jnp.float32
BF16 = jnp.bfloat16
G_ROW, E_ROW, RHO_ROW, W_ROW, ID_ROW, GD_ROW = range(6)


def dg(a, b, ca, cb):
    return lax.dot_general(a, b, (((ca,), (cb,)), ((), ())),
                           precision=lax.Precision.HIGHEST, preferred_element_type=F32)


def nn(a, b):
    return dg(a, b, 1, 0)


def nt(a, b):
    return dg(a, b, 1, 1)


def lane_eye(rows, lanes, shift):
    return (lax.broadcasted_iota(jnp.int32, (rows, lanes), 1)
            == lax.broadcasted_iota(jnp.int32, (rows, lanes), 0) + shift).astype(F32)


def chol_inverse(mat):
    n = mat.shape[0]
    panels = n // 8
    width = 2 * n
    rows = [jnp.concatenate([mat[8 * p:8 * p + 8, :], lane_eye(8, n, 8 * p)], axis=1) for p in range(panels)]
    sub = lax.broadcasted_iota(jnp.int32, (8, width), 0)
    out = []
    for p in range(panels):
        w = rows[p]
        spread = lambda v, k: jnp.broadcast_to(v[:, 8 * p + k:8 * p + k + 1], (8, width))
        d = [spread(w, k) for k in range(8)]
        rest = {q: [spread(rows[q], k) for k in range(8)] for q in range(p + 1, panels)}
        done = jnp.zeros((8, width), F32)
        for k in range(8):
            row_of = lambda v: jnp.broadcast_to(v[k:k + 1, :], (8, width))
            pivot = row_of(d[k])
            inv = 1.0 / pivot
            at_k = sub == k
            w_row = row_of(w)
            done = jnp.where(at_k, w_row * lax.rsqrt(pivot), done)
            scaled = w_row * inv
            factor = d[k]
            w = jnp.where(at_k, scaled, w - factor * scaled)
            for j in range(k + 1, 8):
                d_row = row_of(d[j]) * inv
                d[j] = jnp.where(at_k, d_row, d[j] - factor * d_row)
        out.append(done)
        for q in range(p + 1, panels):
            for k in range(8):
                rows[q] = rows[q] - rest[q][k] * jnp.broadcast_to(w[k:k + 1, :], (8, width))
    return jnp.concatenate(out, axis=0)[:, n:]


def filtered(theta, h21, h22):
    n, m = theta.shape[0], h22.shape[0]
    h12 = h21.T
    whole = jnp.concatenate([jnp.concatenate([h22, h21], axis=1), jnp.concatenate([h12, theta], axis=1)], axis=0)
    inv = 1.0 / jnp.max(jnp.sum(jnp.abs(whole), axis=1, keepdims=True))
    search = lane_eye(n, m + n, m) - whole[m:, :] * inv
    for _ in range(FILTER - 1):
        search = search - nn(search, whole) * inv
    q = nn(chol_inverse(nt(search, search)), search)
    return q[:, m:], q[:, :m], nt(nn(q, whole), q)


def dense0_kernel(scale, gram_ref, coef_ref, theta_ref):
    v = gram_ref.shape[0]
    sbs = gram_ref[:, :v] * scale
    sks = gram_ref[:, v:] * scale
    li = chol_inverse(sbs)
    theta = nt(nn(li, sks), li)
    coef_ref[:, :v] = li
    coef_ref[:, v:] = -nn(theta, li)
    theta_ref[...] = theta


def dense1_kernel(scale, gram_ref, coef_ref, theta_ref, coef1_ref, theta1_ref):
    v = gram_ref.shape[0]
    li = coef_ref[:, :v]
    theta = theta_ref[...]
    rbs, rks, rbr, rkr = [gram_ref[:, i * v:(i + 1) * v] * scale for i in (0, 2, 1, 3)]
    lrx = nt(rbs, li)
    arx = nt(rks, li)
    jr = chol_inverse(rbr - nt(lrx, lrx))
    t = arx - nn(lrx, theta)
    f = rkr - nt(lrx, arx) - nt(t, lrx)
    h21 = nn(jr, t)
    h22 = nt(nn(jr, f), jr)
    qz, qy, ritz = filtered(theta, h21, h22)
    b = nn(qy, jr)
    a = nn(qz - nn(b, lrx), li)
    coef1_ref[:, :v] = a
    coef1_ref[:, v:2 * v] = b
    coef1_ref[:, 2 * v:3 * v] = -nn(ritz, a)
    coef1_ref[:, 3 * v:] = -nn(ritz, b)
    theta1_ref[...] = ritz


def previous_kernel(scale, gram_ref, coef1_ref, out_ref):
    v = gram_ref.shape[0]
    ab = coef1_ref[:, :2 * v]
    b = coef1_ref[:, v:2 * v]
    for i in range(2):
        part = nn(b, gram_ref[:, 2 * i * v:2 * (i + 1) * v] * scale)
        out_ref[:, 2 * i * v:(2 * i + 1) * v] = nt(part, ab)
        out_ref[:, (2 * i + 1) * v:2 * (i + 1) * v] = nt(part[:, v:], b)


def dense2_kernel(scale, gram_ref, prev_ref, coef1_ref, theta1_ref, coef2_ref, theta2_ref):
    v = gram_ref.shape[0]
    both = coef1_ref[:, :2 * v]
    a = coef1_ref[:, :v]
    b = coef1_ref[:, v:2 * v]
    theta = theta1_ref[...]
    lpx, mpp, apx, app = [prev_ref[:, i * v:(i + 1) * v] for i in range(4)]
    lrx = nt(gram_ref[:, :2 * v] * scale, both)
    arx = nt(gram_ref[:, 2 * v:4 * v] * scale, both)
    mrp = nt(gram_ref[:, v:2 * v] * scale, b)
    arp = nt(gram_ref[:, 3 * v:4 * v] * scale, b)
    rbr = gram_ref[:, 4 * v:5 * v] * scale
    rkr = gram_ref[:, 5 * v:] * scale
    jr = chol_inverse(rbr - nt(lrx, lrx))
    low = nt(mrp.T - nt(lpx, lrx), jr)
    jp = chol_inverse(mpp - nt(lpx, lpx) - nt(low, low))
    jpr = -nn(jp, nn(low, jr))
    jb = jnp.concatenate([jnp.concatenate([jr, jnp.zeros((v, v), F32)], axis=1),
                          jnp.concatenate([jpr, jp], axis=1)], axis=0)
    lx = jnp.concatenate([lrx, lpx], axis=0)
    ax = jnp.concatenate([arx, apx], axis=0)
    ab = jnp.concatenate([jnp.concatenate([rkr, arp], axis=1),
                          jnp.concatenate([arp.T, app], axis=1)], axis=0)
    t = ax - nn(lx, theta)
    f = ab - nt(lx, ax) - nt(t, lx)
    h21 = nn(jb, t)
    h22 = nt(nn(jb, f), jb)
    qz, qy, ritz = filtered(theta, h21, h22)
    cb = nn(qy, jb)
    cx = qz - nn(cb, lx)
    coef2_ref[:, :v] = nn(cx, a)
    coef2_ref[:, v:2 * v] = nn(cx + cb[:, v:], b)
    coef2_ref[:, 2 * v:3 * v] = cb[:, :v]
    coef2_ref[:, 3 * v:] = jnp.zeros((v, v), F32)
    theta2_ref[...] = ritz


def split(value):
    high = value.astype(BF16)
    return high, (value - high.astype(F32)).astype(BF16)


def bdot(a, b, cb):
    return lax.dot_general(a, b, (((1,), (cb,)), ((), ())), preferred_element_type=F32)


def mix(coef_high, coef_both, blocks):
    v = coef_high.shape[0]
    pairs = [split(block) for block in blocks]
    high = jnp.concatenate([p[0] for p in pairs], axis=0)
    low = jnp.concatenate([p[1] for p in pairs], axis=0)
    main = bdot(coef_both, high, 0)
    return main[:v] + main[v:] + bdot(coef_high, low, 0)


class Grid:
    def __init__(self, shape, n, ycount):
        self.ysides = 1 if ycount == 2 else 2
        self.v, self.c, self.nx, self.ny, self.nz = shape
        self.n = n
        self.part = self.nz // n
        self.blocks = self.c * self.nx * self.ny
        self.lanes = self.blocks * self.nz
        self.yface = self.c * self.nx * self.nz
        self.zface = self.nz * (-(-self.blocks // self.part))
        self.message = self.lanes // n
        assert self.nz % 128 == 0 and self.nz % n == 0 and n & (n - 1) == 0
        pieces = self.ysides * self.c * self.nx + 2 * (self.zface // self.nz)
        self.columns = max(-(-pieces // n), self.nx * self.ny // n)
        assert self.ny % n == 0 and self.ny % 2 == 0 and self.nx > 1 and self.v % 16 == 0 and self.nx <= 8

    def block(self, c, x, y):
        return (c * self.nx + x) * self.ny + y

    def at(self, j):
        return slice(j * self.nz, (j + 1) * self.nz)

    def group_of(self, rows):
        return lax.broadcasted_iota(jnp.int32, (rows, self.nz), 1) // self.part

    def place_of(self, rows):
        return lax.broadcasted_iota(jnp.int32, (rows, self.nz), 1) % self.part


def turn(value, shift):
    shift %= value.shape[1]
    return pltpu.roll(value, shift, 1) if shift else value


def to_group(gd, value, source, target):
    return pltpu.roll(value, ((target - source) & (gd.n - 1)) * gd.part, 1)


def put_yfaces(gd, my, rows, get, refs):
    for c in range(gd.c):
        for x in range(gd.nx):
            at = gd.at(c * gd.nx + x)
            low, high = get(c, x, 0), get(c, x, gd.ny - 1)
            if gd.ysides == 1:
                refs[0][:rows, at] = jnp.where(my == 0, high, low)
            else:
                refs[0][:rows, at] = low
                refs[1][:rows, at] = high


class Edges:
    def __init__(self, gd, rows):
        self.gd = gd
        columns = gd.zface // gd.nz
        self.low = [jnp.zeros((rows, gd.nz), F32)] * columns
        self.high = [jnp.zeros((rows, gd.nz), F32)] * columns
        self.place = gd.place_of(rows)

    def add(self, value, j, low_turn=0, high_turn=None):
        gd = self.gd
        column, place = j // gd.part, j % gd.part
        here = self.place == place
        high_turn = 1 - gd.part if high_turn is None else high_turn
        self.low[column] = jnp.where(here, turn(value, place + low_turn), self.low[column])
        self.high[column] = jnp.where(here, turn(value, place + high_turn), self.high[column])

    def finish(self, zlo, zhi):
        for i in range(len(self.low)):
            zlo[:, self.gd.at(i)] = self.low[i]
            zhi[:, self.gd.at(i)] = self.high[i]


def stencil(gd, my, get, halo, coef_ref, x, y):
    zb, za = halo[-2:]
    if gd.ysides == 1:
        before = lambda face: jnp.where(my == 0, 0.0, halo[0][:gd.v, face])
        after = lambda face: jnp.where(my == 0, halo[0][:gd.v, face], 0.0)
    else:
        before = lambda face: halo[0][:gd.v, face]
        after = lambda face: halo[1][:gd.v, face]
    row = lambda r, xx, yy: coef_ref[r:r + 1, gd.at(xx * gd.ny + yy)]
    scaled = lambda c, xx, yy: get(c, xx, yy) * row(G_ROW, xx, yy)
    g, e = row(G_ROW, x, y), row(E_ROW, x, y)
    values = [get(c, x, y) for c in range(gd.c)]
    half = 0.5 * functools.reduce(jnp.add, values)
    group, place = gd.group_of(gd.v), gd.place_of(gd.v)
    out = []
    for c in range(gd.c):
        j = gd.block(c, x, y)
        h = values[c] * g
        face = gd.at(c * gd.nx + x)
        if x > 0:
            near = scaled(c, x - 1, y)
        else:
            near = jnp.where(group == 0, 0.0, turn(scaled(c, gd.nx - 1, y), gd.part))
        if x < gd.nx - 1:
            near = near + scaled(c, x + 1, y)
        else:
            near = near + jnp.where(group == gd.n - 1, 0.0, turn(scaled(c, 0, y), -gd.part))
        near = near + (scaled(c, x, y - 1) if y > 0 else before(face))
        near = near + (scaled(c, x, y + 1) if y < gd.ny - 1 else after(face))
        column, at = gd.at(j // gd.part), j % gd.part
        near = near + jnp.where(place == 0, turn(zb[:gd.v, column], -at), turn(h, 1))
        near = near + jnp.where(place == gd.part - 1, turn(za[:gd.v, column], gd.part - 1 - at), turn(h, -1))
        out.append(g * (6.0 * h - near) + e * (values[c] + half))
    return out


def gram_of(left_both, right_high, right_low):
    v = left_both.shape[0] // 2
    main = bdot(left_both[...], right_high[...], 1)
    return main[:v] + main[v:] + bdot(left_both[:v, :], right_low[...], 1)


def scatter(gd, me, rows, pieces, out_refs, at, out_rows=slice(None)):
    group = gd.group_of(rows)
    for s in range(gd.n):
        target = me ^ s
        value = None
        for q in range(gd.n):
            moved = to_group(gd, pieces[q], target, q)
            value = moved if q == 0 else jnp.where(group == q, moved, value)
        out_refs[s][out_rows, at] = value


def gather(gd, me, rows, values, q):
    group = gd.group_of(rows)
    block = None
    for s in range(gd.n):
        source = me ^ s
        moved = to_group(gd, values[s], q, source)
        block = moved if s == 0 else jnp.where(group == source, moved, block)
    return block


def lanes_of(gd, j):
    return pl.ds(pl.multiple_of(j * gd.nz, gd.nz), gd.nz)


def send_kernel(gd, me_ref, *refs):
    sources, messages = refs[:4], refs[4:4 + gd.n]
    yfaces = refs[4 + gd.n:4 + gd.n + gd.ysides]
    zlo, zhi, field_ref, s_ref, sems = refs[4 + gd.n + gd.ysides:]
    me, v, nz, rows = me_ref[0], gd.v, gd.nz, gd.nx * gd.ny
    targets = [s_ref] + [field_ref.at[f * rows:(f + 1) * rows] for f in range(3)]
    copies = [pltpu.make_async_copy(a, b, sems.at[i]) for i, (a, b) in enumerate(zip(sources, targets))]
    for copy in copies:
        copy.start()
    for copy in copies:
        copy.wait()

    def column(i, _):
        scatter(gd, me, v, [s_ref[pl.ds(i * gd.n + q, v, stride=gd.blocks), :] for q in range(gd.n)],
                messages, lanes_of(gd, i))
        return 0

    lax.fori_loop(0, gd.blocks // gd.n, column, 0, unroll=2)
    field = lambda f, r: field_ref[f * rows + r:f * rows + r + 1, :]

    def tall(c, x, y):
        r = x * gd.ny + y
        g = field(0, r)
        w = jnp.broadcast_to(field(2, r) / (6.0 * g * g + 1.5 * field(1, r)), (8, nz))
        return jnp.concatenate([s_ref[pl.ds(gd.block(c, x, y), v, stride=gd.blocks), :] * g, w], axis=0)

    put_yfaces(gd, me_ref[1], v + 8, tall, yfaces)
    edges = Edges(gd, v + 8)
    for x in range(gd.nx):
        for y in range(gd.ny):
            for c in range(gd.c):
                edges.add(tall(c, x, y), gd.block(c, x, y), 1, -gd.part)
    edges.finish(zlo, zhi)


def halo_kernel(gd, me_ref, *refs):
    yfaces = refs[:gd.ysides]
    zlo, zhi, zlo_in, zhi_in, field_ref = refs[gd.ysides:gd.ysides + 5]
    messages = refs[gd.ysides + 5:]
    me, rows, nz = me_ref[0], gd.v + 8, gd.nz
    group = gd.group_of(rows)
    pieces = [ref[:, gd.at(j)] for ref in yfaces for j in range(gd.c * gd.nx)]
    for own, other, at in ((zlo, zlo_in, 0), (zhi, zhi_in, gd.n - 1)):
        pieces += [jnp.where(group == at, other[:, gd.at(i)], own[:, gd.at(i)]) for i in range(gd.zface // nz)]
    pieces += [pieces[-1]] * (gd.columns * gd.n - len(pieces))
    for i in range(gd.columns):
        scatter(gd, me, rows, pieces[gd.n * i:gd.n * (i + 1)], messages, gd.at(i))
    for f in range(3):
        for i in range(gd.nx * gd.ny // gd.n):
            row = f * gd.nx * gd.ny + gd.n * i
            scatter(gd, me, 1, [field_ref[row + q:row + q + 1, :] for q in range(gd.n)], messages, gd.at(i),
                    slice(gd.v + 1 + f, gd.v + 2 + f))


def receive_kernel(gd, me_ref, *refs):
    messages, halo_messages = refs[:gd.n], refs[gd.n:2 * gd.n]
    sm_ref, coef_ref, *halo = refs[2 * gd.n:]
    me, v, nz = me_ref[0], gd.v, gd.nz
    for i in range(gd.nx * gd.ny // gd.n):
        values = [m[v:, gd.at(i)] for m in halo_messages]
        for q in range(gd.n):
            block = gather(gd, me, 8, values, q)
            g, e, rho = (block[k:k + 1] for k in (1, 2, 3))
            inverse = 1.0 / (6.0 * g * g + 1.5 * e)
            for k, value in enumerate((g, e, rho, rho * inverse, inverse, g * inverse)):
                coef_ref[k:k + 1, gd.at(gd.n * i + q)] = value
    targets = [(ref, j) for ref in halo[:-2] for j in range(gd.c * gd.nx)]
    targets += [(ref, i) for ref in halo[-2:] for i in range(gd.zface // nz)]
    for t, (ref, j) in enumerate(targets):
        ref[:, gd.at(j)] = gather(gd, me, v + 8, [m[:, gd.at(t // gd.n)] for m in halo_messages], t % gd.n)

    def column(i, _):
        values = [m[:, lanes_of(gd, i)] for m in messages]
        for q in range(gd.n):
            sm_ref[:, lanes_of(gd, i * gd.n + q)] = gather(gd, me, v, values, q)
        return 0

    lax.fori_loop(0, gd.blocks // gd.n, column, 0, unroll=2)


def image_kernel(gd, me_ref, sm_ref, coef_ref, *refs):
    sides = gd.ysides + 2
    halo, (ks_ref, gram_ref), faces = refs[:sides], refs[sides:sides + 2], refs[sides + 2:2 * sides + 2]
    left, right_high, right_low = refs[2 * sides + 2:]
    v = gd.v
    get = lambda c, x, y: sm_ref[:, gd.at(gd.block(c, x, y))]
    factor = lambda x, y: coef_ref[GD_ROW:GD_ROW + 1, gd.at(x * gd.ny + y)]
    edges = Edges(gd, v)
    for x in range(gd.nx):
        for y in range(gd.ny):
            rho = coef_ref[RHO_ROW:RHO_ROW + 1, gd.at(x * gd.ny + y)]
            images = stencil(gd, me_ref[1], get, halo, coef_ref, x, y)
            for c in range(gd.c):
                at = gd.at(gd.block(c, x, y))
                value = get(c, x, y)
                ks_ref[:, at] = images[c]
                edges.add(images[c] * factor(x, y), gd.block(c, x, y))
                left[:v, at], left[v:, at] = split(value)
                for i, part in enumerate((value * rho, images[c])):
                    right_high[i * v:(i + 1) * v, at], right_low[i * v:(i + 1) * v, at] = split(part)
    edges.finish(*faces[-2:])
    put_yfaces(gd, me_ref[1], v, lambda c, x, y: ks_ref[:, gd.at(gd.block(c, x, y))] * factor(x, y), faces)
    gram_ref[...] = gram_of(left, right_high, right_low)


def residual_kernel(gd, last, depth, me_ref, *refs):
    v, nz = gd.v, gd.nz
    refs = list(refs)
    take = lambda n: [refs.pop(0) for _ in range(n)]
    (mix_ref, coef_ref) = take(2)
    images, vectors = take(depth), take(depth)
    sides = gd.ysides + 2
    image_halo = [take(sides) for _ in range(depth)]
    vector_halo = [take(sides) for _ in range(depth)]
    if last:
        gram_ref, messages = take(1)[0], take(gd.n)
    else:
        r_ref, kr_ref, gram_ref = take(3)
        messages = take(gd.n)
        halo, faces = take(sides), take(sides)
        edges = Edges(gd, v)
    both, left, right_high, right_low = take(4)
    if last:
        r_ref, halo = take(1)[0], take(sides)
    both[:v, :], both[v:, :] = split(mix_ref[...])
    mixed = lambda a, b: mix(both[:v, :], both[...], a + b)
    first = vector_halo[0]

    def interior(c, _):
        for i in range(gd.nx * gd.ny // 2):
            at = pl.ds(pl.multiple_of(c * gd.nx * gd.ny * nz + 2 * i * nz, 2 * nz), 2 * nz)
            row = slice(2 * i * nz, 2 * (i + 1) * nz)
            inverse, w = coef_ref[ID_ROW:ID_ROW + 1, row], coef_ref[W_ROW:W_ROW + 1, row]
            r_ref[:, at] = mixed([ref[:, at] * inverse for ref in images], [ref[:, at] * w for ref in vectors])
        return 0

    for side in range(gd.ysides):
        for j in range(gd.c * gd.nx):
            at = gd.at(j)
            w = first[side][v:v + 1, at]
            halo[side][:, at] = mixed([h[side][:v, at] for h in image_halo], [h[side][:v, at] * w for h in vector_halo])
    for side in (gd.ysides, gd.ysides + 1):
        w = first[side][v:v + 1, :]
        halo[side][...] = mixed([h[side][:v, :] for h in image_halo], [h[side][:v, :] * w for h in vector_halo])
    lax.fori_loop(0, gd.c, interior, 0)
    me = me_ref[0]

    def column(i, _):
        scatter(gd, me, v, [r_ref[:, lanes_of(gd, i * gd.n + q)] for q in range(gd.n)], messages, lanes_of(gd, i))
        return 0

    lax.fori_loop(0, gd.blocks // gd.n, column, 0)
    get = lambda c, x, y: r_ref[:, gd.at(gd.block(c, x, y))]
    for x in range(gd.nx):
        for y in range(gd.ny):
            r = gd.at(x * gd.ny + y)
            rho = coef_ref[RHO_ROW:RHO_ROW + 1, r]
            stiff = stencil(gd, me_ref[1], get, halo, coef_ref, x, y)
            for c in range(gd.c):
                at = gd.at(gd.block(c, x, y))
                value = get(c, x, y)
                if not last:
                    kr_ref[:, at] = stiff[c]
                    edges.add(stiff[c] * coef_ref[GD_ROW:GD_ROW + 1, r], gd.block(c, x, y))
                left[:v, at], left[v:, at] = split(value)
                parts = [ref[:, at] * rho for ref in vectors] + [ref[:, at] for ref in images]
                place = depth if not last else 2 * depth
                parts.insert(place, value * rho)
                parts.append(stiff[c])
                for i, part in enumerate(parts):
                    right_high[i * v:(i + 1) * v, at], right_low[i * v:(i + 1) * v, at] = split(part)
    if not last:
        edges.finish(*faces[-2:])
        put_yfaces(gd, me_ref[1], v, lambda c, x, y: kr_ref[:, gd.at(gd.block(c, x, y))]
                   * coef_ref[GD_ROW:GD_ROW + 1, gd.at(x * gd.ny + y)], faces)
    gram_ref[...] = gram_of(left, right_high, right_low)


def final_kernel(gd, me_ref, mix_ref, *refs):
    parts, (out_ref, both) = [refs[i * gd.n:(i + 1) * gd.n] for i in range(3)], refs[3 * gd.n:]
    me, v = me_ref[0], gd.v
    k = 3 * v
    both[:v, :], both[v:, :] = split(mix_ref[...])
    high, pair = both[:v, :k], both[:, :k]

    def column(i, _):
        at = lanes_of(gd, i)
        value = mix(high, pair, [jnp.concatenate([m[:, at] for m in messages], axis=1) for messages in parts])
        values = [value[:, gd.at(s)] for s in range(gd.n)]
        for q in range(gd.n):
            out_ref[pl.ds(i * gd.n + q, v, stride=gd.blocks), :] = gather(gd, me, v, values, q)
        return 0

    lax.fori_loop(0, gd.blocks // gd.n, column, 0, unroll=3)


def call(kernel, outs, args, scratch=(), flops=1 << 20, vmem=16, scalars=0, free=0):
    vmem_spec = pl.BlockSpec(memory_space=pltpu.VMEM)
    specs = ([pl.BlockSpec(memory_space=pltpu.SMEM)] * scalars + [pl.BlockSpec(memory_space=pl.ANY)] * free
             + [vmem_spec] * (len(args) - scalars - free))
    results = pl.pallas_call(
        kernel,
        out_shape=[jax.ShapeDtypeStruct(s, F32) for s in outs],
        in_specs=specs,
        out_specs=[vmem_spec] * len(outs),
        scratch_shapes=[d if s is None else pltpu.VMEM(s, d) for s, d in scratch],
        compiler_params=pltpu.CompilerParams(vmem_limit_bytes=vmem << 20),
        cost_estimate=pl.CostEstimate(flops=flops, bytes_accessed=1 << 20, transcendentals=0),
    )(*args)
    return list(results)


def exchange(faces):
    nx, ny, nz = (lax.axis_size(a) for a in AXES)
    lines = ((("gx", "gz"), [x * nz + z for z in range(nz) for x in range(nx)]),)
    if ny == 2:
        out = [lax.ppermute(faces[0], "gy", [(0, 1), (1, 0)])]
    else:
        out, lines = [], (("gy", list(range(ny))),) + lines
    for (axes, line), low, high in zip(lines, faces[len(out)::2], faces[len(out) + 1::2]):
        out += both_ways(low, high, axes, line)
    return out


def both_ways(low, high, axes, line):
    up = list(zip(line[:-1], line[1:]))
    return [lax.ppermute(high, axes, up), lax.ppermute(low, axes, [(j, i) for i, j in up])]


def swap(messages):
    n = len(messages)
    return messages[:1] + [lax.ppermute(messages[s], "gx", [(i, i ^ s) for i in range(n)]) for s in range(1, n)]


def sum_over(x, axis):
    n = lax.axis_size(axis)
    if n & (n - 1):
        return lax.psum(x, axis)
    if n <= 4:
        parts = [lax.ppermute(x, axis, [(i, i ^ s) for i in range(n)]) for s in range(1, n)]
        return functools.reduce(jnp.add, parts, x)
    step = 1
    while step < n:
        x = x + lax.ppermute(x, axis, [(i, i ^ step) for i in range(n)])
        step *= 2
    return x


def total(x, later, move):
    n = lax.axis_size("gy")
    me = lax.axis_index("gy")
    half = x.shape[0] // 2
    pair = [(0, 1), (1, 0)]
    piece = lambda k: lax.dynamic_slice_in_dim(x, k * half, half, 0)
    if n == 2:
        mine = piece(me) + lax.ppermute(piece(1 - me), "gy", pair)
    else:
        mine = sum_over(x, "gy")
    mine = sum_over(mine, "gx")
    mine, later = lax.optimization_barrier((mine, later))
    moved = move(later)
    mine = sum_over(mine, "gz")
    if n != 2:
        return mine, moved
    theirs = lax.ppermute(mine, "gy", pair)
    order = [jnp.concatenate(p, 0) for p in ((mine, theirs), (theirs, mine))]
    return jnp.where(me == 0, *order), moved


def local(start_block, stiff_field, shift_field, mass_field):
    n = lax.axis_size("gx")
    gd = Grid(start_block.shape, n, lax.axis_size("gy"))
    v, nz, lanes = gd.v, gd.nz, gd.lanes
    count = stiff_field.size * gd.c
    for axis in AXES:
        count *= lax.axis_size(axis)
    scale = 1.0 / count
    rows = gd.nx * gd.ny
    me = jnp.stack([lax.axis_index("gx"), lax.axis_index("gy")]).astype(jnp.int32)
    fields = [f.reshape(rows, nz) for f in (stiff_field, shift_field, mass_field)]
    native = start_block.reshape(v * gd.blocks, nz)
    faces = [(v, gd.yface)] * gd.ysides + [(v, gd.zface)] * 2
    tall = [(v + 8, gd.yface)] * gd.ysides + [(v + 8, gd.zface)] * 2
    full, square = (v, lanes), (v, v)
    messages = [(v, gd.message)] * n
    part = functools.partial

    *sent, kept = call(part(send_kernel, gd), messages + tall + [(3 * rows, nz)], [me, native] + fields,
                       [((v * gd.blocks, nz), F32), (None, pltpu.SemaphoreType.DMA((4,)))], scalars=1, free=4)
    received = swap(sent[:n])
    yfaces, (zlo, zhi) = sent[n:-2], sent[-2:]
    line = list(range(lax.axis_size("gz")))
    beside = (exchange(yfaces + [zlo, zhi])[:1] if gd.ysides == 1
              else both_ways(*yfaces, "gy", list(range(lax.axis_size("gy")))))
    beside += [zlo, zhi] + both_ways(zhi, zlo, "gz", line)
    around = call(part(halo_kernel, gd), [(v + 8, gd.columns * nz)] * n, [me] + beside + [kept], scalars=1)
    around = swap(around)
    sm, coef, *halo_s = call(part(receive_kernel, gd), [full, (8, rows * nz)] + tall,
                             [me] + received + around, scalars=1)
    gram_scratch = lambda n: [((2 * v, lanes), BF16), ((n * v, lanes), BF16), ((n * v, lanes), BF16)]
    ks, gram0, *faces_u = call(part(image_kernel, gd), [full, (v, 2 * v)] + faces,
                               [me, sm, coef] + halo_s, gram_scratch(2), flops=1 << 32, scalars=1)
    gram0, halo_u = total(gram0, faces_u, exchange)
    coef0, theta0 = call(part(dense0_kernel, scale), [(v, 2 * v), square], [gram0], flops=1 << 31)

    r0, kr0, gram1, *rest = call(part(residual_kernel, gd, False, 1),
                                 [full, full, (v, 4 * v)] + messages + faces + faces,
                                 [me, coef0, coef, ks, sm] + halo_u + halo_s,
                                 [((2 * v, 2 * v), BF16)] + gram_scratch(4), flops=1 << 33, vmem=26, scalars=1)
    r0_sent, halo_r, faces_b = rest[:n], rest[n:n + len(faces)], rest[n + len(faces):]

    def move(a):
        moved = swap(a[0])
        return moved, exchange(a[1])

    gram1, (r0_moved, halo_b) = total(gram1, (r0_sent, faces_b), move)
    coef1, theta1 = call(part(dense1_kernel, scale), [(v, 4 * v), square], [gram1, coef0, theta0],
                         flops=1 << 33)

    gram2, *r1_sent = call(part(residual_kernel, gd, True, 2), [(v, 6 * v)] + messages,
                           [me, coef1, coef, ks, kr0, sm, r0] + halo_u + halo_b + halo_s + halo_r,
                           [((2 * v, 4 * v), BF16)] + gram_scratch(6) + [(full, F32)] + [(f, F32) for f in faces],
                           flops=1 << 33, vmem=32, scalars=1)
    gram2, r1_moved = total(gram2, r1_sent, swap)
    (prev,) = call(part(previous_kernel, scale), [(v, 4 * v)], [gram1, coef1])
    coef2, theta2 = call(part(dense2_kernel, scale), [(v, 4 * v), square], [gram2, prev, coef1, theta1],
                         flops=1 << 33)
    (modes,) = call(part(final_kernel, gd), [(v * gd.blocks, nz)],
                    [me, coef2] + sent[:n] + r0_moved + r1_moved, [((2 * v, 4 * v), BF16)], scalars=1)
    return modes.reshape(start_block.shape), theta2


def solution(mesh):
    grid = P("gx", "gy", "gz")
    block = P(None, None, "gx", "gy", "gz")
    return jax.shard_map(local, mesh=mesh, in_specs=(block, grid, grid, grid), out_specs=(block, P()), check_vma=False)
```

time: 254 us -> 185 us (0.73)
  waiting for transfers between devices: 105 us -> 59.1 us
  local copies, waits for them, and re-layouts: 21.1 us -> 4.73 us
  starting transfers between devices: 66.9 us -> 58.7 us
  Pallas kernels: 56.2 us -> 60.6 us
  other arithmetic: 3.05 us -> 0.18 us
    ppermute x18, waiting for transfers between devices: 72 us -> 17.4 us  [sum_over(): lax.ppermute(x, axis, [(i, i ^ s) for i in range(n)])]
    unnamed x86 -> x32, local copies, waits for them, and re-layouts: 19.6 us -> 4.68 us
    ppermute x24 -> x27, waiting for transfers between devices: 32.6 us -> 41.7 us  [the longest x12 31 us: swap(): lax.ppermute(messages[s], 'gx', [(i, i ^ s) for i in range(n)])]
    ppermute x24 -> x27, starting transfers between devices: 36.9 us -> 31.5 us  [the longest x12 16.1 us: swap(): lax.ppermute(messages[s], 'gx', [(i, i ^ s) for i in range(n)])]
    pallas_call x9 -> x11, Pallas kernels: 56.2 us -> 60.6 us  [call(): pl.pallas_call(kernel, out_shape=[jax.ShapeDtypeStruct(s, F32) for s in o...]
    ppermute x18, starting transfers between devices: 30.1 us -> 27.3 us  [sum_over(): lax.ppermute(x, axis, [(i, i ^ s) for i in range(n)])]
  transfers between devices with their start and end apart: 42 -> 45, of which waited for: 22 -> 26; matrix products, arithmetic and copies ran while one was open for 1% -> 0% of each run, Pallas kernels for 4% -> 13%
where the time goes in v2:
time: 185 us; the launch traced here: 184 us
  Pallas kernels  60.6 us (33%)
  waiting for transfers between devices  59.1 us (32%)
  starting transfers between devices  58.7 us (32%)
  local copies, waits for them, and re-layouts  4.73 us (3%)
    pallas_call x11, Pallas kernels, call(): pl.pallas_call(kernel, out_shape=[jax.ShapeDtypeStruct(s, F32) for s in o...  60.6 us
    ppermute x12, waiting for transfers between devices, swap(): lax.ppermute(messages[s], 'gx', [(i, i ^ s) for i in range(n)])  31 us
    ppermute x18, starting transfers between devices, sum_over(): lax.ppermute(x, axis, [(i, i ^ s) for i in range(n)])  27.3 us
    ppermute x18, waiting for transfers between devices, sum_over(): lax.ppermute(x, axis, [(i, i ^ s) for i in range(n)])  17.4 us
    ppermute x12, starting transfers between devices, swap(): lax.ppermute(messages[s], 'gx', [(i, i ^ s) for i in range(n)])  16.1 us
    ppermute x3, starting transfers between devices, both_ways(): lax.ppermute(high, axes, up)  9.61 us
    ppermute x3, waiting for transfers between devices, both_ways(): lax.ppermute(low, axes, [(j, i) for i, j in up])  7.39 us
    unnamed x32, local copies, waits for them, and re-layouts  4.68 us
  transfers between devices with their start and end apart: 45, of which 26 were waited for; matrix products, arithmetic and copies ran while one was open for 0% of the time, Pallas kernels for 13%

profile of v2, /device:TPU:0, one launch (start us, length us, event | category | flops | bytes accessed | tf_op | source)
XLA Modules:
  0.0 184.3 jit_solution(11674250642121947902)
XLA Ops:
  4.2 3.9 %shard_map.59 = (f32[64,1536]{1,0:T(8,128)S(1)}, f32[64,1536]{1,0:T(8,128)S(1)}, f32[64,1536]{1,0:T(8,128)S(1)}, f32[64,1536]{1,0:T(8,128)S(1)}, f32[72,768]{1,0...) custom-call(s32[2]{0:T(128)S(1)} %pad_add_fusion.me_ref, ...), custom_call_target="tpu_custom_call" | custom-call | flops 1048576 | bytes 1048576 | tf_op jit(solution)/shard_map/pallas_call | solution.py:518
  8.7 4.5 %collective-permute-start.4 = (f32[72,256]{1,0:T(8,128)S(1)}, f32[72,256]{1,0:T(8,128)S(1)}, u32[]{:S(2)}, u32[]{:S(2)}) collective-permute-start(f32[72,256]{1,0:T(8,128)S(1)} %get-tuple-element.70.refs_1_), channel_id=1, source_target_pairs={{0,1},{1,2},{2,3},{4,5},{5,6},{6,7},{8,9},{9,10},{10,11},{12,13},{... | collective-permute-start | bytes 221192 | tf_op jit(solution)/shard_map/ppermute | solution.py:544
  13.2 1.6 collective-permute-start
  18.0 4.9 %collective-permute-done.5.refs_4_ = f32[72,256]{1,0:T(8,128)S(1)} collective-permute-done((f32[72,256]{1,0:T(8,128)S(1)}, f32[72,256]{1,0:T(8,128)S(1)}, u32[]{:S(2)}, u32[]{:S(2)}) %collective-permute-start.5) | collective-permute-done | bytes 73760 | tf_op jit(solution)/shard_map/ppermute | solution.py:544
  23.0 2.0 %shard_map.60 = (f32[72,512]{1,0:T(8,128)S(1)}, f32[72,512]{1,0:T(8,128)S(1)}, f32[72,512]{1,0:T(8,128)}, f32[72,512]{1,0:T(8,128)S(1)}) custom-call(s32[2]{0:T(128)S(1)} %pad_add_fusion.me_ref, f32[72,768]{1,0:T(8,128)S(1)} %collective-permute-done.3.refs_0_, f32[72,256]{1,0:T(8,128)S(1)} %get-tuple-element.70.refs_1_, ...), custom_call_target="tpu_custom_call" | custom-call | flops 1048576 | bytes 1048576 | tf_op jit(solution)/shard_map/pallas_call | solution.py:518
  28.0 8.2 %collective-permute-done.6.refs_5_ = f32[72,512]{1,0:T(8,128)S(1)} collective-permute-done((f32[72,512]{1,0:T(8,128)S(1)}, f32[72,512]{1,0:T(8,128)S(1)}, u32[]{:S(2)}, u32[]{:S(2)}) %collective-permute-start.6) | collective-permute-done | bytes 147488 | tf_op jit(solution)/shard_map/ppermute | solution.py:549
  36.1 2.4 %collective-permute-start.8 = (f32[72,512]{1,0:T(8,128)S(1)}, f32[72,512]{1,0:T(8,128)S(1)}, u32[]{:S(2)}, u32[]{:S(2)}) collective-permute-start(f32[72,512]{1,0:T(8,128)S(1)} %get-tuple-element.76), channel_id=1, source_target_pairs={{0,24},{8,16},{16,8},{24,0},{1,25},{9,17},{17,9},{25,1},{2,26},{10... | collective-permute-start | bytes 442376 | tf_op jit(solution)/shard_map/ppermute | solution.py:549
  38.6 3.6 %collective-permute-done.8.refs_7_ = f32[72,512]{1,0:T(8,128)S(1)} collective-permute-done((f32[72,512]{1,0:T(8,128)S(1)}, f32[72,512]{1,0:T(8,128)S(1)}, u32[]{:S(2)}, u32[]{:S(2)}) %collective-permute-start.8) | collective-permute-done | bytes 147488 | tf_op jit(solution)/shard_map/ppermute | solution.py:549
  42.2 3.1 %shard_map.61 = (f32[64,6144]{1,0:T(8,128)S(1)}, f32[8,2048]{1,0:T(8,128)S(1)}, f32[72,768]{1,0:T(8,128)S(1)}, f32[72,256]{1,0:T(8,128)S(1)}, f32[72,256]{1,0:T(8,128)S(1)}) custom-call(s32[2]{0:T(128)S(1)} %pad_add_fusion.me_ref, f32[64,1536]{1,0:T(8,128)S(1)} %get-tuple-element.65.refs_0_, f32[64,1536]{1,0:T(8,128)S(1)} %collective-permute-done.refs_1_, ...), custom_call_target="tpu_custom_call" | custom-call | flops 1048576 | bytes 1048576 | tf_op jit(solution)/shard_map/pallas_call | solution.py:518
  45.3 5.3 %shard_map.62 = (f32[64,6144]{1,0:T(8,128)S(1)}, f32[64,128]{1,0:T(8,128)S(1)}, f32[64,768]{1,0:T(8,128)S(1)}, f32[64,256]{1,0:T(8,128)}, f32[64,256]{1,0:T(8,128)}) custom-call(s32[2]{0:T(128)S(1)} %pad_add_fusion.me_ref, f32[64,6144]{1,0:T(8,128)S(1)} %get-tuple-element.77.sm_ref.refs_3_.refs_4_, f32[8,2048]{1,0:T(8,128)S(1)} %get-tuple-element.78.coef_ref.refs_1_, ...), custom_call_target="tpu_custom_call" | custom-call | flops 4294967296 | bytes 1048576 | tf_op jit(solution)/shard_map/pallas_call | solution.py:518
  53.0 2.4 %collective-permute-start.12 = (f32[32,128]{1,0:T(8,128)S(1)}, f32[32,128]{1,0:T(8,128)S(1)}, u32[]{:S(2)}, u32[]{:S(2)}) collective-permute-start(f32[32,128]{1,0:T(8,128)S(1)} %dynamic-slice_add_fusion.2), channel_id=1, source_target_pairs={{0,24},{8,16},{16,8},{24,0},{1,25},{9,17},{17,9},{25,1},{2,26},{10... | collective-permute-start | bytes 49160 | tf_op jit(solution)/shard_map/ppermute | solution.py:557
  59.7 1.9 %collective-permute-start.15 = (f32[32,128]{1,0:T(8,128)S(1)}, f32[32,128]{1,0:T(8,128)S(1)}, u32[]{:S(2)}, u32[]{:S(2)}) collective-permute-start(f32[32,128]{1,0:T(8,128)S(1)} %add_add_fusion.5), channel_id=1, source_target_pairs={{0,3},{1,2},{2,1},{3,0},{4,7},{5,6},{6,5},{7,4},{8,11},{9,10},{10,... | collective-permute-start | bytes 49160 | tf_op jit(solution)/shard_map/ppermute | solution.py:557
  66.5 2.4 %collective-permute-start.18 = (f32[64,256]{1,0:T(8,128)}, f32[64,256]{1,0:T(8,128)S(1)}, u32[]{:S(2)}, u32[]{:S(2)}) collective-permute-start(f32[64,256]{1,0:T(8,128)} %get-tuple-element.90), channel_id=1, source_target_pairs={{0,8},{8,16},{16,24},{24,1},{1,9},{9,17},{17,25},{25,2},{2,10},{10... | collective-permute-start | bytes 196616 | tf_op jit(solution)/shard_map/ppermute | solution.py:544
  70.7 2.7 %shard_map.63 = (f32[64,128]{1,0:T(8,128)S(1)}, f32[64,64]{1,0:T(8,128)S(1)}) custom-call(f32[64,128]{1,0:T(8,128)S(1)} %maximum_select_fusion.2.gram_ref), custom_call_target="tpu_custom_call" | custom-call | flops 2147483648 | bytes 1048576 | tf_op jit(solution)/shard_map/pallas_call | solution.py:518
  73.5 2.4 %collective-permute-done.19.refs_6_.refs_8_ = f32[64,256]{1,0:T(8,128)S(1)} collective-permute-done((f32[64,256]{1,0:T(8,128)}, f32[64,256]{1,0:T(8,128)S(1)}, u32[]{:S(2)}, u32[]{:S(2)}) %collective-permute-start.19) | collective-permute-done | bytes 65568 | tf_op jit(solution)/shard_map/ppermute | solution.py:544
  76.0 9.4 %shard_map.64 = (f32[64,6144]{1,0:T(8,128)S(1)}, f32[64,6144]{1,0:T(8,128)S(1)}, f32[64,256]{1,0:T(8,128)S(1)}, f32[64,1536]{1,0:T(8,128)S(1)}, f32[64,1536]{1,0...) custom-call(s32[2]{0:T(128)S(1)} %pad_add_fusion.me_ref, ...), custom_call_target="tpu_custom_call" | custom-call | flops 8589934592 | bytes 1048576 | tf_op jit(solution)/shard_map/pallas_call | solution.py:518
  86.7 4.3 %collective-permute-start.23 = (f32[32,256]{1,0:T(8,128)S(1)}, f32[32,256]{1,0:T(8,128)S(1)}, u32[]{:S(2)}, u32[]{:S(2)}) collective-permute-start(f32[32,256]{1,0:T(8,128)S(1)} %dynamic-slice_add_fusion.1), channel_id=1, source_target_pairs={{0,24},{8,16},{16,8},{24,0},{1,25},{9,17},{17,9},{25,1},{2,26},{10... | collective-permute-start | bytes 98312 | tf_op jit(solution)/shard_map/ppermute | solution.py:557
  92.9 2.0 %collective-permute-done.22 = f32[32,256]{1,0:T(8,128)S(1)} collective-permute-done((f32[32,256]{1,0:T(8,128)S(1)}, f32[32,256]{1,0:T(8,128)S(1)}, u32[]{:S(2)}, u32[]{:S(2)}) %collective-permute-start.22) | collective-permute-done | bytes 32800 | tf_op jit(solution)/shard_map/ppermute | solution.py:557
  95.0 2.4 %collective-permute-start.26 = (f32[32,256]{1,0:T(8,128)S(1)}, f32[32,256]{1,0:T(8,128)S(1)}, u32[]{:S(2)}, u32[]{:S(2)}) collective-permute-start(f32[32,256]{1,0:T(8,128)S(1)} %add_add_fusion.3), channel_id=1, source_target_pairs={{0,3},{1,2},{2,1},{3,0},{4,7},{5,6},{6,5},{7,4},{8,11},{9,10},{10,... | collective-permute-start | bytes 98312 | tf_op jit(solution)/shard_map/ppermute | solution.py:557
  97.7 1.8 collective-permute-start.24
  102.3 2.7 %collective-permute-start.29 = (f32[64,256]{1,0:T(8,128)S(1)}, f32[64,256]{1,0:T(8,128)S(1)}, u32[]{:S(2)}, u32[]{:S(2)}) collective-permute-start(f32[64,256]{1,0:T(8,128)S(1)} %get-tuple-element.106), channel_id=1, source_target_pairs={{0,8},{8,16},{16,24},{24,1},{1,9},{9,17},{17,25},{25,2},{2,10},{10... | collective-permute-start | bytes 196616 | tf_op jit(solution)/shard_map/ppermute | solution.py:544
  106.5 7.3 %shard_map.65 = (f32[64,256]{1,0:T(8,128)S(1)}, f32[64,64]{1,0:T(8,128)S(1)}) custom-call(f32[64,256]{1,0:T(8,128)S(1)} %maximum_select_fusion.1.gram_ref, f32[64,128]{1,0:T(8,128)S(1)} %get-tuple-element.87.refs_0_.coef_ref, f32[64,64]{1,0:T(8,128)S(1)} %get-tuple-element.101.theta_ref), custom_call_target="tpu_custom_call" | custom-call | flops 8589934592 | bytes 1048576 | tf_op jit(solution)/shard_map/pallas_call | solution.py:518
  113.8 10.8 %shard_map.66 = (f32[64,384]{1,0:T(8,128)S(1)}, f32[64,1536]{1,0:T(8,128)S(1)}, f32[64,1536]{1,0:T(8,128)S(1)}, f32[64,1536]{1,0:T(8,128)S(1)}, f32[64,1536]{1,0:T(8,128)S(1)}) custom-call(s32[2]{0:T(128)S(1)} %pad_add_fusion.me_ref, f32[64,256]{1,0:T(8,128)S(1)} %get-tuple-element.102.refs_0_.coef1_ref, f32[8,2048]{1,0:T(8,128)S(1)} %copy-done.13, ...), custom_call_target="tpu_custom_call" | custom-call | flops 8589934592 | bytes 1048576 | tf_op jit(solution)/shard_map/pallas_call | solution.py:518
  126.0 3.5 %collective-permute-start.34 = (f32[32,384]{1,0:T(8,128)S(1)}, f32[32,384]{1,0:T(8,128)S(1)}, u32[]{:S(2)}, u32[]{:S(2)}) collective-permute-start(f32[32,384]{1,0:T(8,128)S(1)} %dynamic-slice_add_fusion), channel_id=1, source_target_pairs={{0,24},{8,16},{16,8},{24,0},{1,25},{9,17},{17,9},{25,1},{2,26},{10... | collective-permute-start | bytes 147464 | tf_op jit(solution)/shard_map/ppermute | solution.py:557
  131.6 1.9 %collective-permute-done.33 = f32[32,384]{1,0:T(8,128)S(1)} collective-permute-done((f32[32,384]{1,0:T(8,128)S(1)}, f32[32,384]{1,0:T(8,128)S(1)}, u32[]{:S(2)}, u32[]{:S(2)}) %collective-permute-start.33) | collective-permute-done | bytes 49184 | tf_op jit(solution)/shard_map/ppermute | solution.py:557
  134.6 2.6 %collective-permute-start.37 = (f32[32,384]{1,0:T(8,128)S(1)}, f32[32,384]{1,0:T(8,128)S(1)}, u32[]{:S(2)}, u32[]{:S(2)}) collective-permute-start(f32[32,384]{1,0:T(8,128)S(1)} %add_add_fusion.1), channel_id=1, source_target_pairs={{0,3},{1,2},{2,1},{3,0},{4,7},{5,6},{6,5},{7,4},{8,11},{9,10},{10,... | collective-permute-start | bytes 147464 | tf_op jit(solution)/shard_map/ppermute | solution.py:557
  140.9 1.8 %collective-permute-done.36 = f32[32,384]{1,0:T(8,128)S(1)} collective-permute-done((f32[32,384]{1,0:T(8,128)S(1)}, f32[32,384]{1,0:T(8,128)S(1)}, u32[]{:S(2)}, u32[]{:S(2)}) %collective-permute-start.36) | collective-permute-done | bytes 49184 | tf_op jit(solution)/shard_map/ppermute | solution.py:557
  143.9 2.4 %collective-permute-start.41 = (f32[64,1536]{1,0:T(8,128)S(1)}, f32[64,1536]{1,0:T(8,128)S(1)}, u32[]{:S(2)}, u32[]{:S(2)}) collective-permute-start(f32[64,1536]{1,0:T(8,128)S(1)} %get-tuple-element.122), channel_id=1, source_target_pairs={{0,24},{8,16},{16,8},{24,0},{1,25},{9,17},{17,9},{25,1},{2,26},{10... | collective-permute-start | bytes 1179656 | tf_op jit(solution)/shard_map/ppermute | solution.py:549
  151.3 10.6 %shard_map.68 = (f32[64,256]{1,0:T(8,128)S(1)}, f32[64,64]{1,0:T(8,128)}) custom-call(f32[64,384]{1,0:T(8,128)S(1)} %maximum_select_fusion.gram_ref, f32[64,256]{1,0:T(8,128)S(1)} %shard_map.67.prev_ref, f32[64,256]{1,0:T(8,128)S(1)} %get-tuple-element.102.refs_0_.coef1_ref, f32[64,64]{1,0:T(8,128)S(1)} %get-tuple-element.117.theta1_ref), custom_call_target="tpu_custom_call" | custom-call | flops 8589934592 | bytes 1048576 | tf_op jit(solution)/shard_map/pallas_call | solution.py:518
  163.3 3.3 %collective-permute-done.42.refs_9_ = f32[64,1536]{1,0:T(8,128)S(1)} collective-permute-done((f32[64,1536]{1,0:T(8,128)S(1)}, f32[64,1536]{1,0:T(8,128)S(1)}, u32[]{:S(2)}, u32[]{:S(2)}) %collective-permute-start.42) | collective-permute-done | bytes 393248 | tf_op jit(solution)/shard_map/ppermute | solution.py:549
  166.6 13.0 %collective-permute-done.43.refs_10_ = f32[64,1536]{1,0:T(8,128)S(1)} collective-permute-done((f32[64,1536]{1,0:T(8,128)S(1)}, f32[64,1536]{1,0:T(8,128)S(1)}, u32[]{:S(2)}, u32[]{:S(2)}) %collective-permute-start.43) | collective-permute-done | bytes 393248 | tf_op jit(solution)/shard_map/ppermute | solution.py:549
  179.6 4.7 %shard_map.69 = f32[3072,128]{1,0:T(8,128)} custom-call(s32[2]{0:T(128)S(1)} %pad_add_fusion.me_ref, f32[64,256]{1,0:T(8,128)S(1)} %get-tuple-element.118.mix_ref, f32[64,1536]{1,0:T(8,128)S(1)} %get-tuple-element.65.refs_0_, f32[64,1536]{1,0:T(8,128)S(1)} %get-tuple-element.66.refs_1_, f32[64,1536]{1,0:T(8,128)S(1)} %get-tuple-element.67.refs_2_, ...), custom_call_target="tpu_custom_call" | custom-call | flops 1048576 | bytes 1048576 | tf_op jit(solution)/shard_map/pallas_call | solution.py:518
  (117 shorter events, 47.5 us)
Async XLA Ops:
  8.1 14.8 %collective-permute-start.3 = (f32[72,768]{1,0:T(8,128)S(1)}, f32[72,768]{1,0:T(8,128)S(1)}, u32[]{:S(2)}, u32[]{:S(2)}) collective-permute-start(f32[72,768]{1,0:T(8,128)S(1)} %get-tuple-element.69), channel_id=1, source_target_pairs={{0,4},{4,0},{1,5},{5,1},{2,6},{6,2},{3,7},{7,3},{8,12},{12,8},{9,1... | collective-permute-start | bytes 663560 | tf_op jit(solution)/shard_map/ppermute | solution.py:534
  8.7 8.0 %collective-permute-start.4 = (f32[72,256]{1,0:T(8,128)S(1)}, f32[72,256]{1,0:T(8,128)S(1)}, u32[]{:S(2)}, u32[]{:S(2)}) collective-permute-start(f32[72,256]{1,0:T(8,128)S(1)} %get-tuple-element.70.refs_1_), channel_id=1, source_target_pairs={{0,1},{1,2},{2,3},{4,5},{5,6},{6,7},{8,9},{9,10},{10,11},{12,13},{... | collective-permute-start | bytes 221192 | tf_op jit(solution)/shard_map/ppermute | solution.py:544
  13.2 29.0 %collective-permute-start = (f32[64,1536]{1,0:T(8,128)S(1)}, f32[64,1536]{1,0:T(8,128)S(1)}, u32[]{:S(2)}, u32[]{:S(2)}) collective-permute-start(f32[64,1536]{1,0:T(8,128)S(1)} %get-tuple-element.66.refs_1_), channel_id=1, source_target_pairs={{0,8},{8,0},{16,24},{24,16},{1,9},{9,1},{17,25},{25,17},{2,10},{10... | collective-permute-start | bytes 1179656 | tf_op jit(solution)/shard_map/ppermute | solution.py:549
  14.8 27.4 %collective-permute-start.1 = (f32[64,1536]{1,0:T(8,128)S(1)}, f32[64,1536]{1,0:T(8,128)S(1)}, u32[]{:S(2)}, u32[]{:S(2)}) collective-permute-start(f32[64,1536]{1,0:T(8,128)S(1)} %get-tuple-element.67.refs_2_), channel_id=1, source_target_pairs={{0,16},{8,24},{16,0},{24,8},{1,17},{9,25},{17,1},{25,9},{2,18},{10... | collective-permute-start | bytes 1179656 | tf_op jit(solution)/shard_map/ppermute | solution.py:549
  16.3 25.9 %collective-permute-start.2 = (f32[64,1536]{1,0:T(8,128)S(1)}, f32[64,1536]{1,0:T(8,128)S(1)}, u32[]{:S(2)}, u32[]{:S(2)}) collective-permute-start(f32[64,1536]{1,0:T(8,128)S(1)} %get-tuple-element.68.refs_3_), channel_id=1, source_target_pairs={{0,24},{8,16},{16,8},{24,0},{1,25},{9,17},{17,9},{25,1},{2,26},{10... | collective-permute-start | bytes 1179656 | tf_op jit(solution)/shard_map/ppermute | solution.py:549
  16.8 6.2 %collective-permute-start.5 = (f32[72,256]{1,0:T(8,128)S(1)}, f32[72,256]{1,0:T(8,128)S(1)}, u32[]{:S(2)}, u32[]{:S(2)}) collective-permute-start(f32[72,256]{1,0:T(8,128)S(1)} %get-tuple-element.71.refs_2_), channel_id=1, source_target_pairs={{1,0},{2,1},{3,2},{5,4},{6,5},{7,6},{9,8},{10,9},{11,10},{13,12},{... | collective-permute-start | bytes 221192 | tf_op jit(solution)/shard_map/ppermute | solution.py:544
  25.0 11.2 %collective-permute-start.6 = (f32[72,512]{1,0:T(8,128)S(1)}, f32[72,512]{1,0:T(8,128)S(1)}, u32[]{:S(2)}, u32[]{:S(2)}) collective-permute-start(f32[72,512]{1,0:T(8,128)S(1)} %get-tuple-element.74), channel_id=1, source_target_pairs={{0,8},{8,0},{16,24},{24,16},{1,9},{9,1},{17,25},{25,17},{2,10},{10... | collective-permute-start | bytes 442376 | tf_op jit(solution)/shard_map/ppermute | solution.py:549
  26.4 12.1 %collective-permute-start.7 = (f32[72,512]{1,0:T(8,128)}, f32[72,512]{1,0:T(8,128)S(1)}, u32[]{:S(2)}, u32[]{:S(2)}) collective-permute-start(f32[72,512]{1,0:T(8,128)} %get-tuple-element.75), channel_id=1, source_target_pairs={{0,16},{8,24},{16,0},{24,8},{1,17},{9,25},{17,1},{25,9},{2,18},{10... | collective-permute-start | bytes 442376 | tf_op jit(solution)/shard_map/ppermute | solution.py:549
  36.1 6.0 %collective-permute-start.8 = (f32[72,512]{1,0:T(8,128)S(1)}, f32[72,512]{1,0:T(8,128)S(1)}, u32[]{:S(2)}, u32[]{:S(2)}) collective-permute-start(f32[72,512]{1,0:T(8,128)S(1)} %get-tuple-element.76), channel_id=1, source_target_pairs={{0,24},{8,16},{16,8},{24,0},{1,25},{9,17},{17,9},{25,1},{2,26},{10... | collective-permute-start | bytes 442376 | tf_op jit(solution)/shard_map/ppermute | solution.py:549
  53.0 4.6 %collective-permute-start.12 = (f32[32,128]{1,0:T(8,128)S(1)}, f32[32,128]{1,0:T(8,128)S(1)}, u32[]{:S(2)}, u32[]{:S(2)}) collective-permute-start(f32[32,128]{1,0:T(8,128)S(1)} %dynamic-slice_add_fusion.2), channel_id=1, source_target_pairs={{0,24},{8,16},{16,8},{24,0},{1,25},{9,17},{17,9},{25,1},{2,26},{10... | collective-permute-start | bytes 49160 | tf_op jit(solution)/shard_map/ppermute | solution.py:557
  59.7 5.5 %collective-permute-start.15 = (f32[32,128]{1,0:T(8,128)S(1)}, f32[32,128]{1,0:T(8,128)S(1)}, u32[]{:S(2)}, u32[]{:S(2)}) collective-permute-start(f32[32,128]{1,0:T(8,128)S(1)} %add_add_fusion.5), channel_id=1, source_target_pairs={{0,3},{1,2},{2,1},{3,0},{4,7},{5,6},{6,5},{7,4},{8,11},{9,10},{10,... | collective-permute-start | bytes 49160 | tf_op jit(solution)/shard_map/ppermute | solution.py:557
  61.6 4.6 %collective-permute-start.14 = (f32[32,128]{1,0:T(8,128)S(1)}, f32[32,128]{1,0:T(8,128)S(1)}, u32[]{:S(2)}, u32[]{:S(2)}) collective-permute-start(f32[32,128]{1,0:T(8,128)S(1)} %add_add_fusion.5), channel_id=1, source_target_pairs={{0,2},{1,3},{2,0},{3,1},{4,6},{5,7},{6,4},{7,5},{8,10},{9,11},{10,... | collective-permute-start | bytes 49160 | tf_op jit(solution)/shard_map/ppermute | solution.py:557
  66.5 7.0 %collective-permute-start.18 = (f32[64,256]{1,0:T(8,128)}, f32[64,256]{1,0:T(8,128)S(1)}, u32[]{:S(2)}, u32[]{:S(2)}) collective-permute-start(f32[64,256]{1,0:T(8,128)} %get-tuple-element.90), channel_id=1, source_target_pairs={{0,8},{8,16},{16,24},{24,1},{1,9},{9,17},{17,25},{25,2},{2,10},{10... | collective-permute-start | bytes 196616 | tf_op jit(solution)/shard_map/ppermute | solution.py:544
  68.9 7.0 %collective-permute-start.19 = (f32[64,256]{1,0:T(8,128)}, f32[64,256]{1,0:T(8,128)S(1)}, u32[]{:S(2)}, u32[]{:S(2)}) collective-permute-start(f32[64,256]{1,0:T(8,128)} %get-tuple-element.91), channel_id=1, source_target_pairs={{8,0},{16,8},{24,16},{1,24},{9,1},{17,9},{25,17},{2,25},{10,2},{18... | collective-permute-start | bytes 196616 | tf_op jit(solution)/shard_map/ppermute | solution.py:544
  70.4 5.5 %collective-permute-start.17 = (f32[64,768]{1,0:T(8,128)S(1)}, f32[64,768]{1,0:T(8,128)S(1)}, u32[]{:S(2)}, u32[]{:S(2)}) collective-permute-start(f32[64,768]{1,0:T(8,128)S(1)} %get-tuple-element.89), channel_id=1, source_target_pairs={{0,4},{4,0},{1,5},{5,1},{2,6},{6,2},{3,7},{7,3},{8,12},{12,8},{9,1... | collective-permute-start | bytes 589832 | tf_op jit(solution)/shard_map/ppermute | solution.py:534
  86.7 6.2 %collective-permute-start.23 = (f32[32,256]{1,0:T(8,128)S(1)}, f32[32,256]{1,0:T(8,128)S(1)}, u32[]{:S(2)}, u32[]{:S(2)}) collective-permute-start(f32[32,256]{1,0:T(8,128)S(1)} %dynamic-slice_add_fusion.1), channel_id=1, source_target_pairs={{0,24},{8,16},{16,8},{24,0},{1,25},{9,17},{17,9},{25,1},{2,26},{10... | collective-permute-start | bytes 98312 | tf_op jit(solution)/shard_map/ppermute | solution.py:557
  95.0 6.0 %collective-permute-start.26 = (f32[32,256]{1,0:T(8,128)S(1)}, f32[32,256]{1,0:T(8,128)S(1)}, u32[]{:S(2)}, u32[]{:S(2)}) collective-permute-start(f32[32,256]{1,0:T(8,128)S(1)} %add_add_fusion.3), channel_id=1, source_target_pairs={{0,3},{1,2},{2,1},{3,0},{4,7},{5,6},{6,5},{7,4},{8,11},{9,10},{10,... | collective-permute-start | bytes 98312 | tf_op jit(solution)/shard_map/ppermute | solution.py:557
  97.3 4.8 %collective-permute-start.25 = (f32[32,256]{1,0:T(8,128)S(1)}, f32[32,256]{1,0:T(8,128)S(1)}, u32[]{:S(2)}, u32[]{:S(2)}) collective-permute-start(f32[32,256]{1,0:T(8,128)S(1)} %add_add_fusion.3), channel_id=1, source_target_pairs={{0,2},{1,3},{2,0},{3,1},{4,6},{5,7},{6,4},{7,5},{8,10},{9,11},{10,... | collective-permute-start | bytes 98312 | tf_op jit(solution)/shard_map/ppermute | solution.py:557
  97.7 4.5 %collective-permute-start.24 = (f32[32,256]{1,0:T(8,128)S(1)}, f32[32,256]{1,0:T(8,128)S(1)}, u32[]{:S(2)}, u32[]{:S(2)}) collective-permute-start(f32[32,256]{1,0:T(8,128)S(1)} %add_add_fusion.3), channel_id=1, source_target_pairs={{0,1},{1,0},{2,3},{3,2},{4,5},{5,4},{6,7},{7,6},{8,9},{9,8},{10,11... | collective-permute-start | bytes 98312 | tf_op jit(solution)/shard_map/ppermute | solution.py:557
  102.3 11.6 %collective-permute-start.29 = (f32[64,256]{1,0:T(8,128)S(1)}, f32[64,256]{1,0:T(8,128)S(1)}, u32[]{:S(2)}, u32[]{:S(2)}) collective-permute-start(f32[64,256]{1,0:T(8,128)S(1)} %get-tuple-element.106), channel_id=1, source_target_pairs={{0,8},{8,16},{16,24},{24,1},{1,9},{9,17},{17,25},{25,2},{2,10},{10... | collective-permute-start | bytes 196616 | tf_op jit(solution)/shard_map/ppermute | solution.py:544
  105.0 8.9 %collective-permute-start.30 = (f32[64,256]{1,0:T(8,128)S(1)}, f32[64,256]{1,0:T(8,128)S(1)}, u32[]{:S(2)}, u32[]{:S(2)}) collective-permute-start(f32[64,256]{1,0:T(8,128)S(1)} %get-tuple-element.107), channel_id=1, source_target_pairs={{8,0},{16,8},{24,16},{1,24},{9,1},{17,9},{25,17},{2,25},{10,2},{18... | collective-permute-start | bytes 196616 | tf_op jit(solution)/shard_map/ppermute | solution.py:544
  106.3 7.6 %collective-permute-start.28 = (f32[64,768]{1,0:T(8,128)S(1)}, f32[64,768]{1,0:T(8,128)S(1)}, u32[]{:S(2)}, u32[]{:S(2)}) collective-permute-start(f32[64,768]{1,0:T(8,128)S(1)} %get-tuple-element.105), channel_id=1, source_target_pairs={{0,4},{4,0},{1,5},{5,1},{2,6},{6,2},{3,7},{7,3},{8,12},{12,8},{9,1... | collective-permute-start | bytes 589832 | tf_op jit(solution)/shard_map/ppermute | solution.py:534
  126.0 5.7 %collective-permute-start.34 = (f32[32,384]{1,0:T(8,128)S(1)}, f32[32,384]{1,0:T(8,128)S(1)}, u32[]{:S(2)}, u32[]{:S(2)}) collective-permute-start(f32[32,384]{1,0:T(8,128)S(1)} %dynamic-slice_add_fusion), channel_id=1, source_target_pairs={{0,24},{8,16},{16,8},{24,0},{1,25},{9,17},{17,9},{25,1},{2,26},{10... | collective-permute-start | bytes 147464 | tf_op jit(solution)/shard_map/ppermute | solution.py:557
  134.6 6.3 %collective-permute-start.37 = (f32[32,384]{1,0:T(8,128)S(1)}, f32[32,384]{1,0:T(8,128)S(1)}, u32[]{:S(2)}, u32[]{:S(2)}) collective-permute-start(f32[32,384]{1,0:T(8,128)S(1)} %add_add_fusion.1), channel_id=1, source_target_pairs={{0,3},{1,2},{2,1},{3,0},{4,7},{5,6},{6,5},{7,4},{8,11},{9,10},{10,... | collective-permute-start | bytes 147464 | tf_op jit(solution)/shard_map/ppermute | solution.py:557
  137.1 5.6 %collective-permute-start.36 = (f32[32,384]{1,0:T(8,128)S(1)}, f32[32,384]{1,0:T(8,128)S(1)}, u32[]{:S(2)}, u32[]{:S(2)}) collective-permute-start(f32[32,384]{1,0:T(8,128)S(1)} %add_add_fusion.1), channel_id=1, source_target_pairs={{0,2},{1,3},{2,0},{3,1},{4,6},{5,7},{6,4},{7,5},{8,10},{9,11},{10,... | collective-permute-start | bytes 147464 | tf_op jit(solution)/shard_map/ppermute | solution.py:557
  138.0 4.7 %collective-permute-start.35 = (f32[32,384]{1,0:T(8,128)S(1)}, f32[32,384]{1,0:T(8,128)S(1)}, u32[]{:S(2)}, u32[]{:S(2)}) collective-permute-start(f32[32,384]{1,0:T(8,128)S(1)} %add_add_fusion.1), channel_id=1, source_target_pairs={{0,1},{1,0},{2,3},{3,2},{4,5},{5,4},{6,7},{7,6},{8,9},{9,8},{10,11... | collective-permute-start | bytes 147464 | tf_op jit(solution)/shard_map/ppermute | solution.py:557
  139.0 10.7 %collective-permute-start.39 = (f32[64,1536]{1,0:T(8,128)S(1)}, f32[64,1536]{1,0:T(8,128)S(1)}, u32[]{:S(2)}, u32[]{:S(2)}) collective-permute-start(f32[64,1536]{1,0:T(8,128)S(1)} %get-tuple-element.120), channel_id=1, source_target_pairs={{0,8},{8,0},{16,24},{24,16},{1,9},{9,1},{17,25},{25,17},{2,10},{10... | collective-permute-start | bytes 1179656 | tf_op jit(solution)/shard_map/ppermute | solution.py:549
  142.8 20.5 %collective-permute-start.40 = (f32[64,1536]{1,0:T(8,128)S(1)}, f32[64,1536]{1,0:T(8,128)S(1)}, u32[]{:S(2)}, u32[]{:S(2)}) collective-permute-start(f32[64,1536]{1,0:T(8,128)S(1)} %get-tuple-element.121), channel_id=1, source_target_pairs={{0,16},{8,24},{16,0},{24,8},{1,17},{9,25},{17,1},{25,9},{2,18},{10... | collective-permute-start | bytes 1179656 | tf_op jit(solution)/shard_map/ppermute | solution.py:549
  143.9 19.4 %collective-permute-start.41 = (f32[64,1536]{1,0:T(8,128)S(1)}, f32[64,1536]{1,0:T(8,128)S(1)}, u32[]{:S(2)}, u32[]{:S(2)}) collective-permute-start(f32[64,1536]{1,0:T(8,128)S(1)} %get-tuple-element.122), channel_id=1, source_target_pairs={{0,24},{8,16},{16,8},{24,0},{1,25},{9,17},{17,9},{25,1},{2,26},{10... | collective-permute-start | bytes 1179656 | tf_op jit(solution)/shard_map/ppermute | solution.py:549
  147.0 19.6 %collective-permute-start.42 = (f32[64,1536]{1,0:T(8,128)S(1)}, f32[64,1536]{1,0:T(8,128)S(1)}, u32[]{:S(2)}, u32[]{:S(2)}) collective-permute-start(f32[64,1536]{1,0:T(8,128)S(1)} %get-tuple-element.124), channel_id=1, source_target_pairs={{0,8},{8,0},{16,24},{24,16},{1,9},{9,1},{17,25},{25,17},{2,10},{10... | collective-permute-start | bytes 1179656 | tf_op jit(solution)/shard_map/ppermute | solution.py:549
  147.2 32.4 %collective-permute-start.43 = (f32[64,1536]{1,0:T(8,128)S(1)}, f32[64,1536]{1,0:T(8,128)S(1)}, u32[]{:S(2)}, u32[]{:S(2)}) collective-permute-start(f32[64,1536]{1,0:T(8,128)S(1)} %get-tuple-element.125), channel_id=1, source_target_pairs={{0,16},{8,24},{16,0},{24,8},{1,17},{9,25},{17,1},{25,9},{2,18},{10... | collective-permute-start | bytes 1179656 | tf_op jit(solution)/shard_map/ppermute | solution.py:549
  149.7 29.9 %collective-permute-start.44 = (f32[64,1536]{1,0:T(8,128)S(1)}, f32[64,1536]{1,0:T(8,128)S(1)}, u32[]{:S(2)}, u32[]{:S(2)}) collective-permute-start(f32[64,1536]{1,0:T(8,128)S(1)} %get-tuple-element.126), channel_id=1, source_target_pairs={{0,24},{8,16},{16,8},{24,0},{1,25},{9,17},{17,9},{25,1},{2,26},{10... | collective-permute-start | bytes 1179656 | tf_op jit(solution)/shard_map/ppermute | solution.py:549
  (29 other events, 107.1 us)
